TPU v7x, 256 devices: a whole 4x4x8 slice. The times are simulated.
256 devices in a mesh: section: 4 (over x_hi, core), expert: 64 (over x_lo, z, y).
Axes of the slice: x: 4 (x_hi: 2, x_lo: 2; x = x_hi * 2 + x_lo), y: 4, z: 8, core: 2. Of those that a mesh axis runs over, the one named last changes fastest.
Arguments:
- x_fwd: bfloat16 [4, 8192, 3584], P('section', 'expert'), may hold values from -6 to 6
- routes_fwd: int32 [4, 8192, 2], P('section', 'expert'), may hold values from 0 to 31, all different within a row; in each aligned block of 128 rows (0 to 127, 128 to 255, ..., all dimensions but the last counted through in order) at most 12 rows name the same one
- affinity_fwd: float32 [4, 8192, 2], P('section', 'expert'), may hold values from 0.1 to 1
- x_bwd: bfloat16 [4, 8192, 3584], P('section', 'expert'), may hold values from -6 to 6
- grad_bwd: bfloat16 [4, 8192, 3584], P('section', 'expert'), may hold values from -6 to 6
- routes_bwd: int32 [4, 8192, 2], P('section', 'expert'), may hold values from 0 to 31, all different within a row; in each aligned block of 128 rows (0 to 127, 128 to 255, ..., all dimensions but the last counted through in order) at most 12 rows name the same one
- affinity_bwd: float32 [4, 8192, 2], P('section', 'expert'), may hold values from 0.1 to 1
- up_weight: bfloat16 [4, 3584, 32768], P('section', None, 'expert'), may hold values from -0.09375 to 0.09375
- down_weight: bfloat16 [4, 32768, 3584], P('section', 'expert'), may hold values from -0.1875 to 0.1875
Outputs:
- fwd_next: bfloat16 [4, 8192, 3584], P('section', 'expert')
- bwd_next: bfloat16 [4, 8192, 3584], P('section', 'expert')
Inputs may be any that keep to these rules, and one draw needn't show every extreme that they name: `routes_fwd`: each row names 2 different experts; in each section, among the 128 rows of one device (aligned blocks), no expert is named more than 12 times, a bound that some block reaches. `routes_bwd`: each row names 2 different experts; in each section, among the 128 rows of one device (aligned blocks), no expert is named more than 12 times, a bound that some block reaches.
All inputs are finite; a program needn't handle non-finite values.
Results may differ from a plain program's by a relative error of at most 0.0041.
Values may be sent and summed in bfloat16 or wider, within the bound.
No kernel may reach another device: no remote copies, remote signals or barrier semaphores. Data moves between devices by JAX's collectives and lax.ppermute only.
A program may use at most 128 MiB of HBM per device.

v0:
```python
import jax
import jax.numpy as jnp
from jax import lax
from jax.sharding import PartitionSpec as P


def from_partner_2(block, axis, apart):
    count = lax.axis_size(axis)
    route = []
    for low in range(count):
        high = low | 1 << apart
        if high != low and high < count:
            route += [(low, high), (high, low)]
    return lax.ppermute(block, axis, route)


def shifted(shard, axis, by):
    size = lax.axis_size(axis)
    return lax.ppermute(shard, axis, [(i, (i + by) % size) for i in range(size)])


def silu_grad(values):
    sigma = jax.nn.sigmoid(values)
    return sigma * (1.0 + values * (1.0 - sigma))


def slot_table(routes, experts, capacity):
    flat_routes = routes.reshape(-1)
    entries = flat_routes.shape[0]
    onehot = (flat_routes[:, None] == jnp.arange(experts, dtype=jnp.int32)[None, :]).astype(
        jnp.int32
    )
    before = jnp.cumsum(onehot, 0) - onehot
    position = jnp.sum(before * onehot, 1)
    slot_of = flat_routes * capacity + position
    source = (
        jnp.full((experts * capacity,), entries, jnp.int32)
        .at[slot_of]
        .set(jnp.arange(entries, dtype=jnp.int32))
    )
    return (slot_of, source)


def serve_rows(received, up_half, down_half):
    sources = received.shape[0]
    slots = received.shape[2]
    model_width = received.shape[3]
    row_count = sources * slots
    rows_fwd = received[:, 0].reshape(row_count, model_width)
    rows_saved = received[:, 1].reshape(row_count, model_width)
    rows_grad = received[:, 2].reshape(row_count, model_width)
    against_rows = (((1,), (1,)), ((), ()))
    hidden = jax.nn.silu(jnp.dot(rows_fwd, up_half, preferred_element_type=jnp.float32)).astype(
        jnp.bfloat16
    )
    part_fwd = jnp.dot(hidden, down_half, preferred_element_type=jnp.float32).astype(jnp.bfloat16)
    pre_act = jnp.dot(rows_saved, up_half, preferred_element_type=jnp.float32)
    hidden_grad = lax.dot_general(
        rows_grad, down_half, against_rows, preferred_element_type=jnp.float32
    )
    pre_grad = (hidden_grad * silu_grad(pre_act)).astype(jnp.bfloat16)
    part_bwd = lax.dot_general(
        pre_grad, up_half, against_rows, preferred_element_type=jnp.float32
    ).astype(jnp.bfloat16)
    return jnp.stack(
        [
            part_fwd.reshape(sources, slots, model_width),
            part_bwd.reshape(sources, slots, model_width),
        ],
        1,
    )


def combine(inputs, routed_rows, affinity):
    tokens = inputs.shape[0]
    top_count = affinity.shape[1]
    weights = affinity / jnp.sum(affinity, -1, keepdims=True)
    routed = routed_rows.reshape(tokens, top_count, inputs.shape[1]).astype(jnp.float32)
    return (inputs.astype(jnp.float32) + jnp.sum(weights[..., None] * routed, 1)).astype(
        jnp.bfloat16
    )


def per_device(
    x_fwd,
    routes_fwd,
    affinity_fwd,
    x_bwd,
    grad_bwd,
    routes_bwd,
    affinity_bwd,
    up_weight,
    down_weight,
):
    devices = lax.axis_size("expert")
    experts = devices // 2
    tokens = x_fwd.shape[1]
    model_width = x_fwd.shape[2]
    top_count = routes_fwd.shape[2]
    capacity = 3 * tokens * top_count // devices
    half_slots = capacity // 2
    up_half = up_weight[0]
    down_half = down_weight[0]
    slot_fwd, source_fwd = slot_table(routes_fwd[0], experts, capacity)
    slot_bwd, source_bwd = slot_table(routes_bwd[0], experts, capacity)
    zero_row = jnp.zeros((1, model_width), jnp.bfloat16)
    row_table = jnp.concatenate([x_fwd[0], zero_row, x_bwd[0], zero_row, grad_bwd[0], zero_row], 0)
    stride = tokens + 1
    token_fwd = (source_fwd // top_count).reshape(experts, capacity)
    token_bwd = (source_bwd // top_count).reshape(experts, capacity)
    gather_index = jnp.stack([token_fwd, token_bwd + stride, token_bwd + 2 * stride], 1)
    send_index = (
        gather_index.reshape(experts, 3, 2, half_slots)
        .transpose(0, 2, 1, 3)
        .reshape(devices, 3, half_slots)
    )
    outgoing = row_table[send_index]
    received = lax.all_to_all(outgoing, "expert", split_axis=0, concat_axis=0, tiled=True)
    partner = from_partner_2(received, "expert", 0)
    result = serve_rows(jnp.concatenate([received, partner], 2), up_half, down_half)
    piece_slots = received.shape[2]
    from_partner = from_partner_2(result[:, :, piece_slots:], "expert", 0)
    summed = (
        result[:, :, :piece_slots].astype(jnp.float32) + from_partner.astype(jnp.float32)
    ).astype(jnp.bfloat16)
    returned = lax.all_to_all(summed, "expert", split_axis=0, concat_axis=0, tiled=True)
    flat_back = returned.reshape(-1, model_width)

    def back_index(slot_of, member):
        expert_id = slot_of // capacity
        within = slot_of % capacity
        return (
            (2 * expert_id + within // half_slots) * 2 + member
        ) * half_slots + within % half_slots

    index_fwd = back_index(slot_fwd, 0)
    index_bwd = back_index(slot_bwd, 1)
    layer_out = combine(x_fwd[0], flat_back[index_fwd], affinity_fwd[0])
    input_grad = combine(grad_bwd[0], flat_back[index_bwd], affinity_bwd[0])
    fwd_next = shifted(layer_out[None], "section", 1)
    bwd_next = shifted(input_grad[None], "section", -1)
    return (fwd_next, bwd_next)


def solution(mesh):
    in_specs = (
        P("section", "expert", None),
        P("section", "expert", None),
        P("section", "expert", None),
        P("section", "expert", None),
        P("section", "expert", None),
        P("section", "expert", None),
        P("section", "expert", None),
        P("section", None, "expert"),
        P("section", "expert", None),
    )
    out_specs = (P("section", "expert", None), P("section", "expert", None))
    return jax.shard_map(
        per_device, mesh=mesh, in_specs=in_specs, out_specs=out_specs, check_vma=False
    )
```

profile of v0, /device:TPU:24, one launch (start us, length us, event | category | flops | bytes accessed | tf_op | source)
XLA Modules:
  0.0 942.5 jit_solution(5526965452766263269)
XLA Ops:
  0.6 0.8 copy.68
  1.7 0.7 broadcast_multiply_fusion
  2.4 0.8 copy.64
  3.5 0.7 broadcast_multiply_fusion.1
  4.1 0.6 reduce-window.16
  5.4 1.4 scatter_custom_fusion.1
  6.9 0.6 reduce-window.14
  8.1 1.4 scatter_custom_fusion
  10.2 15.5 %concatenate.9 = bf16[387,3584]{1,0:T(8,128)(2,1)S(1)} concatenate(bf16[128,3584]{1,0:T(8,128)(2,1)} %bitcast.85, bf16[1,3584]{1,0:T(2,128)(2,1)S(1)} %broadcast_in_dim.2, bf16[128,3584]{1,0:T(8,128)(2,1)} %bitcast.86, bf16[1,3584]{1,0:T(2,128)(2,1)S(1)} %broadcast_in_dim.2, bf16[128,3584]{1,0:T(8,128)(2,1)} %bitcast.84, bf16[1,3584]{1,0:T(2,128)(2,1)S(1)} %broadcast_in_dim.2), dimensions={0} | concatenate | bytes 5548032 | tf_op jit(solution)/shard_map/concatenate | solution.py:107
  25.8 7.5 gather_fusion
  33.3 13.3 %reshape.417 = bf16[64,3,6,3584]{3,2,1,0:T(8,128)(2,1)} reshape(bf16[1152,3584]{1,0:T(8,128)(2,1)} %gather_fusion) | data formatting | bytes 16515072 | tf_op jit(solution)/shard_map/gather | solution.py:117
  46.6 255.6 %all_to_all.10 = bf16[64,3,6,3584]{3,2,1,0:T(8,128)(2,1)} all-to-all(bf16[64,3,6,3584]{3,2,1,0:T(8,128)(2,1)} %reshape.417), channel_id=1, replica_groups=mesh['section'=4,'expert'=64] {'expert'}, dimensions={0} | all-to-all | bytes 16515072 | tf_op jit(solution)/shard_map/all_to_all | solution.py:118
  302.2 10.0 %copy.72 = bf16[64,3,6,3584]{3,0,2,1:T(8,128)(2,1)} copy(bf16[64,3,6,3584]{3,2,1,0:T(8,128)(2,1)} %all_to_all.10) | data formatting | bytes 16515072 | tf_op jit(solution)/shard_map/all_to_all | solution.py:118
  312.3 178.9 %collective-permute-done = bf16[64,3,6,3584]{3,0,2,1:T(8,128)(2,1)} collective-permute-done((bf16[64,3,6,3584]{3,0,2,1:T(8,128)(2,1)}, bf16[64,3,6,3584]{3,0,2,1:T(8,128)(2,1)}, u32[]{:S(2)}, u32[]{:S(2)}) %collective-permute-start) | collective-permute-done | bytes 8257568 | tf_op jit(solution)/shard_map/ppermute | solution.py:14
  491.2 12.1 %copy.73 = bf16[64,3,6,3584]{3,2,1,0:T(8,128)(2,1)} copy(bf16[64,3,6,3584]{3,0,2,1:T(8,128)(2,1)} %collective-permute-done) | data formatting | bytes 16515072 | tf_op jit(solution)/shard_map/ppermute | solution.py:14
  503.2 15.6 %fusion = (bf16[64,1,12,3584]{3,2,1,0:T(8,128)(2,1)}, bf16[64,1,12,3584]{3,2,1,0:T(8,128)(2,1)}, bf16[64,1,12,3584]{3,2,1,0:T(8,128)(2,1)}) fusion(bf16[64,3,6,3584]{3,2,1,0:T(8,128)(2,1)} %all_to_all.10, bf16[64,3,6,3584]{3,2,1,0:T(8,128)(2,1)} %copy.73), kind=kLoop, calls=%fused_computation.10 | loop fusion | flops 33030144 | bytes 33030144 | tf_op jit(solution)/shard_map/concatenate | solution.py:120
  518.9 9.4 reshape_squeeze.13
  528.2 9.4 reshape_squeeze.12
  537.6 6.2 fusion.6
  544.0 3.3 multiply_convert_fusion
  547.3 4.9 convolution_convert_fusion
  552.2 9.3 stack_reshape.11
  561.5 9.4 reshape_squeeze.11
  570.8 7.0 multiply_convert_fusion.1
  577.8 4.8 convolution_convert_fusion.1
  582.7 9.6 %stack_reshape.10 = bf16[64,1,12,3584]{3,2,0,1:T(8,128)(2,1)} reshape(bf16[768,3584]{1,0:T(8,128)(2,1)} %convolution_convert_fusion.1) | data formatting | bytes 11010048 | tf_op jit(solution)/shard_map/stack;reshape | solution.py:65
  592.3 6.2 copy_dynamic-update-slice_fusion.1
  598.5 3.0 copy_dynamic-update-slice_fusion
  601.6 3.3 slice.59
  604.9 2.5 copy-done
  607.7 118.7 %collective-permute-done.1 = bf16[64,2,6,3584]{3,0,2,1:T(8,128)(2,1)S(1)} collective-permute-done((bf16[64,2,6,3584]{3,0,2,1:T(8,128)(2,1)}, bf16[64,2,6,3584]{3,0,2,1:T(8,128)(2,1)S(1)}, u32[]{:S(2)}, u32[]{:S(2)}) %collective-permute-start.1) | collective-permute-done | bytes 5505056 | tf_op jit(solution)/shard_map/ppermute | solution.py:14
  726.4 4.1 add_convert_fusion
  730.5 11.4 %copy.76 = bf16[64,2,6,3584]{3,1,2,0:T(2,128)(2,1)} copy(bf16[64,2,6,3584]{3,0,2,1:T(8,128)(2,1)S(1)} %add_convert_fusion) | data formatting | bytes 11010048 | tf_op jit(solution)/shard_map/convert_element_type | solution.py:125
  741.9 7.1 all-to-all-start.1
  749.3 120.9 %all-to-all-done.1 = bf16[64,2,6,3584]{3,1,2,0:T(2,128)(2,1)} async-done(((bf16[64,2,6,3584]{3,1,2,0:T(2,128)(2,1)}), bf16[64,2,6,3584]{3,1,2,0:T(2,128)(2,1)}, u32[]{:S(2)}, u32[]{:S(2)}) %all-to-all-start.1) | async-done | bytes 5505056 | tf_op jit(solution)/shard_map/all_to_all | solution.py:126
  870.2 7.3 copy.77
  877.5 9.7 %reshape.413 = bf16[768,3584]{1,0:T(8,128)(2,1)} reshape(bf16[64,2,6,3584]{3,2,1,0:T(8,128)(2,1)} %copy.77) | data formatting | bytes 11010048 | tf_op jit(solution)/shard_map/reshape | solution.py:127
  887.2 6.8 gather_fusion.2
  894.0 3.7 reshape.415
  897.7 7.3 multiply_reduce_fusion
  905.0 1.1 fusion.10
  906.1 0.5 collective-permute-start.3
  906.6 6.8 gather_fusion.1
  913.5 3.7 reshape.414
  917.2 7.3 multiply_reduce_fusion.1
  924.8 14.3 %collective-permute-done.2 = bf16[1,128,3584]{2,1,0:T(8,128)(2,1)S(1)} collective-permute-done((bf16[1,128,3584]{2,1,0:T(8,128)(2,1)S(1)}, bf16[1,128,3584]{2,1,0:T(8,128)(2,1)S(1)}, u32[]{:S(2)}, u32[]{:S(2)}) %collective-permute-start.2) | collective-permute-done | bytes 917536 | tf_op jit(solution)/shard_map/ppermute | solution.py:19
  939.1 0.9 copy.90
  940.1 2.2 copy.91
  (72 shorter events, 3.7 us)
Async XLA Ops:
  312.1 179.1 %collective-permute-start = (bf16[64,3,6,3584]{3,0,2,1:T(8,128)(2,1)}, bf16[64,3,6,3584]{3,0,2,1:T(8,128)(2,1)}, u32[]{:S(2)}, u32[]{:S(2)}) collective-permute-start(bf16[64,3,6,3584]{3,0,2,1:T(8,128)(2,1)} %copy.72), channel_id=1, source_target_pairs={{0,1},{1,0},{2,3},{3,2},{4,5},{5,4},{6,7},{7,6},{8,9},{9,8},{10,11... | collective-permute-start | bytes 24772616 | tf_op jit(solution)/shard_map/ppermute | solution.py:14
  537.6 6.2 copy-start.1
  537.6 6.3 copy-start.7
  544.0 3.3 copy-start.6
  570.8 7.0 copy-start.8
  582.6 15.9 %slice-start = ((s8[7340032]{0:T(1024)(128)(4,1)}), s8[3145728]{0:T(1024)(128)(4,1)S(1)}, s32[]{:S(2)}) async-start(s8[7340032]{0:T(1024)(128)(4,1)} %bitcast.82), calls=%async_computation.2 | async-start | bytes 6291456
  592.3 6.3 slice-start.1
  601.6 5.9 copy-start
  607.4 119.0 %collective-permute-start.1 = (bf16[64,2,6,3584]{3,0,2,1:T(8,128)(2,1)}, bf16[64,2,6,3584]{3,0,2,1:T(8,128)(2,1)S(1)}, u32[]{:S(2)}, u32[]{:S(2)}) collective-permute-start(bf16[64,2,6,3584]{3,0,2,1:T(8,128)(2,1)} %slice.59), channel_id=1, source_target_pairs={{0,1},{1,0},{2,3},{3,2},{4,5},{5,4},{6,7},{7,6},{8,9},{9,8},{10,11... | collective-permute-start | bytes 16515080 | tf_op jit(solution)/shard_map/ppermute | solution.py:14
  741.9 7.2 copy-start.4
  741.9 7.3 copy-start.5
  741.9 128.4 %all-to-all-start.1 = ((bf16[64,2,6,3584]{3,1,2,0:T(2,128)(2,1)}), bf16[64,2,6,3584]{3,1,2,0:T(2,128)(2,1)}, u32[]{:S(2)}, u32[]{:S(2)}) async-start(bf16[64,2,6,3584]{3,1,2,0:T(2,128)(2,1)} %copy.76), calls=%async_computation.1 | async-start | bytes 11010048 | tf_op jit(solution)/shard_map/all_to_all | solution.py:126
  894.0 11.0 %copy-start.2 = (bf16[1,128,3584]{2,1,0:T(8,128)(2,1)S(1)}, bf16[1,128,3584]{2,1,0:T(8,128)(2,1)}, u32[]{:S(2)}) copy-start(bf16[1,128,3584]{2,1,0:T(8,128)(2,1)} %param.13) | copy-start | bytes 2752516
  906.1 18.7 %collective-permute-start.3 = (bf16[1,128,3584]{2,1,0:T(8,128)(2,1)}, bf16[1,128,3584]{2,1,0:T(8,128)(2,1)}, u32[]{:S(2)}, u32[]{:S(2)}) collective-permute-start(bf16[1,128,3584]{2,1,0:T(8,128)(2,1)} %fusion.10), channel_id=1, source_target_pairs={{0,192},{64,0},{128,64},{192,128},{1,193},{65,1},{129,65},{193,129... | collective-permute-start | bytes 2752520 | tf_op jit(solution)/shard_map/ppermute | solution.py:19
  913.5 11.1 %copy-start.3 = (bf16[1,128,3584]{2,1,0:T(8,128)(2,1)S(1)}, bf16[1,128,3584]{2,1,0:T(8,128)(2,1)}, u32[]{:S(2)}) copy-start(bf16[1,128,3584]{2,1,0:T(8,128)(2,1)} %param.9) | copy-start | bytes 2752516
  924.7 14.4 %collective-permute-start.2 = (bf16[1,128,3584]{2,1,0:T(8,128)(2,1)S(1)}, bf16[1,128,3584]{2,1,0:T(8,128)(2,1)S(1)}, u32[]{:S(2)}, u32[]{:S(2)}) collective-permute-start(bf16[1,128,3584]{2,1,0:T(8,128)(2,1)S(1)} %fusion.11), channel_id=1, source_target_pairs={{0,64},{64,128},{128,192},{192,0},{1,65},{65,129},{129,193},{193,1... | collective-permute-start | bytes 2752520 | tf_op jit(solution)/shard_map/ppermute | solution.py:19
where the time goes:
time: 952 us; the launch traced here: 942 us
  waiting for transfers between devices  433 us (45%)
  blocking collectives  256 us (27%)
  local copies, waits for them, and re-layouts  180 us (19%)
  other arithmetic  38.7 us (4%)
  matrix products  26.2 us (3%)
    ppermute x2, waiting for transfers between devices, from_partner_2(): return lax.ppermute(block, axis, route)  298 us
    all_to_all x1, blocking collectives, per_device(): lax.all_to_all(outgoing, 'expert', split_axis=0, concat_axis=0, tiled=True)  256 us
    all_to_all x1, waiting for transfers between devices, per_device(): lax.all_to_all(summed, 'expert', split_axis=0, concat_axis=0, tiled=True)  121 us
    another operation x3, local copies, waits for them, and re-layouts, serve_rows(): jnp.stack([part_fwd.reshape(sources, slots, model_width), part_bwd.reshap...  21.9 us
    gather x2, local copies, waits for them, and re-layouts, per_device(): outgoing = row_table[send_index]  20.8 us
  transfers between devices with their start and end apart: 5, of which 4 were waited for; matrix products, arithmetic and copies ran while one was open for 2% of the time, Pallas kernels for 0%

commit v1 on v0

v1 whole, which is shorter than its diff:
```python
import functools

import jax
import jax.numpy as jnp
from jax import lax
from jax.experimental import pallas as pl
from jax.experimental.pallas import tpu as pltpu
from jax.sharding import PartitionSpec as P

VMEM = pl.BlockSpec(memory_space=pltpu.VMEM)


def same_side_groups(devices):
    sides = [0 if d % 4 in (0, 3) else 1 for d in range(devices)]
    return [[d for d in range(devices) if sides[d] == side] for side in (0, 1)]


def from_partner(block, axis):
    count = lax.axis_size(axis)
    return lax.ppermute(block, axis, [(i, i ^ 1) for i in range(count)])


def shifted(shard, axis, by):
    size = lax.axis_size(axis)
    return lax.ppermute(shard, axis, [(i, (i + by) % size) for i in range(size)])


def silu_grad(values):
    sigma = jax.nn.sigmoid(values)
    return sigma * (1.0 + values * (1.0 - sigma))


def place_of(routes, experts):
    tokens = routes.shape[1]
    expert_id = lax.broadcasted_iota(jnp.int32, (experts, tokens), 0)
    named = (expert_id == routes[0:1, :]) | (expert_id == routes[1:2, :])
    earlier = (
        lax.broadcasted_iota(jnp.int32, (tokens, tokens), 0)
        < lax.broadcasted_iota(jnp.int32, (tokens, tokens), 1)
    )
    before = jnp.dot(
        named.astype(jnp.float32).astype(jnp.bfloat16),
        earlier.astype(jnp.float32).astype(jnp.bfloat16),
        preferred_element_type=jnp.float32,
    )
    return jnp.where(named, before, -1.0)


def slot_rows(place, block, first, capacity):
    experts, tokens = place.shape
    rows = experts * block
    row = lax.broadcasted_iota(jnp.int32, (rows, experts), 0)
    col = lax.broadcasted_iota(jnp.int32, (rows, experts), 1)
    begin = col * block + first
    mine = (row >= begin) & (row < begin + capacity)
    spread = mine.astype(jnp.float32).astype(jnp.bfloat16)
    within = jnp.sum(jnp.where(mine, row - begin + 1, 0).astype(jnp.float32), 1, keepdims=True) - 1.0
    slot = jnp.dot(
        spread, (place + 1.0).astype(jnp.bfloat16), preferred_element_type=jnp.float32
    ) - 1.0
    return (slot == within) & (within >= 0.0)


def as_bf16(mask):
    return mask.astype(jnp.float32).astype(jnp.bfloat16)


def dispatch_fwd_kernel(capacity, experts, routes_ref, x_ref, out_ref):
    place = place_of(routes_ref[...], experts)
    pick = as_bf16(slot_rows(place, capacity, 0, capacity))
    rows = jnp.dot(pick, x_ref[...], preferred_element_type=jnp.float32)
    out_ref[...] = rows.reshape(out_ref.shape).astype(jnp.bfloat16)


def dispatch_bwd_kernel(capacity, experts, routes_ref, x_ref, g_ref, out_ref):
    place = place_of(routes_ref[...], experts)
    pick_x = as_bf16(slot_rows(place, 2 * capacity, 0, capacity))
    pick_g = as_bf16(slot_rows(place, 2 * capacity, capacity, capacity))
    rows = jnp.dot(pick_x, x_ref[...], preferred_element_type=jnp.float32)
    rows = rows + jnp.dot(pick_g, g_ref[...], preferred_element_type=jnp.float32)
    out_ref[...] = rows.astype(jnp.bfloat16)


def combine_kernel(capacity, experts, routes_ref, affinity_ref, x_ref, back_ref, out_ref):
    routes = routes_ref[...]
    affinity = affinity_ref[...]
    tokens = routes.shape[1]
    rows = experts * capacity
    pick = slot_rows(place_of(routes, experts), capacity, 0, capacity)
    row = lax.broadcasted_iota(jnp.int32, (rows, tokens), 0)
    weights = affinity / jnp.sum(affinity, 0, keepdims=True)
    back = back_ref[...].reshape(rows, x_ref.shape[1])
    total = x_ref[...].astype(jnp.float32)
    for k in range(2):
        begin = routes[k : k + 1, :] * capacity
        mine = pick & (row >= begin) & (row < begin + capacity)
        picked = lax.dot_general(
            as_bf16(mine), back, (((0,), (0,)), ((), ())), preferred_element_type=jnp.float32
        )
        weight = jnp.broadcast_to(weights[k : k + 1, :], (tokens, tokens)).T[:, 0:1]
        total = total + weight * picked
    out_ref[...] = total.astype(jnp.bfloat16)


def per_device(
    x_fwd,
    routes_fwd,
    affinity_fwd,
    x_bwd,
    grad_bwd,
    routes_bwd,
    affinity_bwd,
    up_weight,
    down_weight,
):
    devices = lax.axis_size("expert")
    experts = devices // 2
    tokens = x_fwd.shape[1]
    model_width = x_fwd.shape[2]
    top_count = routes_fwd.shape[2]
    capacity = 3 * tokens * top_count // devices
    rows = experts * capacity
    groups = same_side_groups(devices)
    params = pltpu.CompilerParams(vmem_limit_bytes=60 * 1024 * 1024)

    up_own = up_weight[0]
    down_own = down_weight[0]
    up_other = from_partner(up_own, "expert")
    down_other = from_partner(down_own, "expert")

    routes_f = routes_fwd[0].T
    routes_b = routes_bwd[0].T

    def exchange(block):
        return lax.all_to_all(
            block, "expert", split_axis=0, concat_axis=0, tiled=True, axis_index_groups=groups
        )

    send_f = pl.pallas_call(
        functools.partial(dispatch_fwd_kernel, capacity, experts),
        out_shape=jax.ShapeDtypeStruct((rows // 4, 4, model_width), jnp.bfloat16),
        in_specs=[VMEM] * 2,
        out_specs=VMEM,
        compiler_params=params,
        name="dispatch_fwd",
    )(routes_f, x_fwd[0])
    recv_f = exchange(send_f)
    send_b = pl.pallas_call(
        functools.partial(dispatch_bwd_kernel, capacity, experts),
        out_shape=jax.ShapeDtypeStruct((2 * rows, model_width), jnp.bfloat16),
        in_specs=[VMEM] * 3,
        out_specs=VMEM,
        compiler_params=params,
        name="dispatch_bwd",
    )(routes_b, x_bwd[0], grad_bwd[0])
    recv_b = exchange(send_b)

    f32 = jnp.float32
    against_rows = (((1,), (1,)), ((), ()))

    x_rows = recv_f.reshape(rows, model_width)
    part = None
    for up, down in ((up_own, down_own), (up_other, down_other)):
        hidden = jax.nn.silu(jnp.dot(x_rows, up, preferred_element_type=f32)).astype(jnp.bfloat16)
        product = jnp.dot(hidden, down, preferred_element_type=f32)
        part = product if part is None else part + product
    back_f = exchange(part.astype(jnp.bfloat16).reshape(rows // 4, 4, model_width))

    blocks = recv_b.reshape(experts, 2 * capacity, model_width)
    x_rows = blocks[:, :capacity].reshape(rows, model_width)
    g_rows = blocks[:, capacity:].reshape(rows, model_width)
    part = None
    for up, down in ((up_own, down_own), (up_other, down_other)):
        pre_act = jnp.dot(x_rows, up, preferred_element_type=f32)
        hidden_grad = lax.dot_general(g_rows, down, against_rows, preferred_element_type=f32)
        pre_grad = (hidden_grad * silu_grad(pre_act)).astype(jnp.bfloat16)
        product = lax.dot_general(pre_grad, up, against_rows, preferred_element_type=f32)
        part = product if part is None else part + product
    back_b = exchange(part.astype(jnp.bfloat16).reshape(rows // 4, 4, model_width))

    def combine(routes, affinity, x, back, name):
        return pl.pallas_call(
            functools.partial(combine_kernel, capacity, experts),
            out_shape=jax.ShapeDtypeStruct((tokens, model_width), jnp.bfloat16),
            in_specs=[VMEM] * 4,
            out_specs=VMEM,
            compiler_params=params,
            name=name,
        )(routes, affinity, x, back)

    layer_out = combine(routes_f, affinity_fwd[0].T, x_fwd[0], back_f, "combine_fwd")
    fwd_next = shifted(layer_out[None], "section", 1)
    input_grad = combine(routes_b, affinity_bwd[0].T, grad_bwd[0], back_b, "combine_bwd")
    bwd_next = shifted(input_grad[None], "section", -1)
    return (fwd_next, bwd_next)


def solution(mesh):
    rows = P("section", "expert", None)
    in_specs = (rows,) * 7 + (P("section", None, "expert"), rows)
    return jax.shard_map(
        per_device, mesh=mesh, in_specs=in_specs, out_specs=(rows, rows), check_vma=False
    )
```

time: 952 us -> 428 us (0.45)
  blocking collectives: 256 us -> 0 us
  waiting for transfers between devices: 433 us -> 278 us
  local copies, waits for them, and re-layouts: 180 us -> 33.3 us
  other arithmetic: 38.7 us -> 0 us
  starting transfers between devices: 8.18 us -> 39.6 us
  matrix products: 26.2 us -> 48.2 us
  Pallas kernels: 0 us -> 20.4 us
    all_to_all x1 -> x0, blocking collectives: 256 us -> none  [per_device(): lax.all_to_all(outgoing, 'expert', split_axis=0, concat_axis=0, tiled=True)]
    ppermute x2, waiting for transfers between devices: 298 us -> 145 us  [from_partner(): return lax.ppermute(block, axis, [(i, i ^ 1) for i in range(count)])]
    another operation x12 -> x0, local copies, waits for them, and re-layouts: 50.3 us -> none  [the longest x3 21.9 us: serve_rows(): jnp.stack([part_fwd.reshape(sources, slots, model_width), part_bwd.reshap...]
    gather x4 -> x0, local copies, waits for them, and re-layouts: 34.4 us -> none  [the longest x2 20.8 us: per_device(): outgoing = row_table[send_index]]
    all_to_all x1 -> x4, starting transfers between devices: 7.14 us -> 37.5 us  [exchange(): lax.all_to_all(block, 'expert', split_axis=0, concat_axis=0, tiled=True,...]
    dot_general x5 -> x6, matrix products: 26.2 us -> 48.2 us  [the longest x2 20 us: per_device(): lax.dot_general(pre_grad, up, against_rows, preferred_element_type=f32)]
    pallas_call x0 -> x4, Pallas kernels: none -> 20.4 us  [the longest x2 9.06 us: combine(): pl.pallas_call(functools.partial(combine_kernel, capacity, experts), out_...]
    convert_element_type x3 -> x0, local copies, waits for them, and re-layouts: 18.7 us -> none  [the longest x1 11.4 us: per_device(): summed = (result[:, :, :piece_slots].astype(jnp.float32) + from_partner.a...]
  transfers between devices with their start and end apart: 5 -> 8, of which waited for: 4 -> 6; matrix products, arithmetic and copies ran while one was open for 2% -> 19% of each run, Pallas kernels for 0% -> 4%
where the time goes in v1:
time: 428 us; the launch traced here: 420 us
  waiting for transfers between devices  278 us (65%)
  matrix products  48.2 us (11%)
  starting transfers between devices  39.6 us (9%)
  local copies, waits for them, and re-layouts  33.3 us (8%)
  Pallas kernels  20.4 us (5%)
    ppermute x2, waiting for transfers between devices, from_partner(): return lax.ppermute(block, axis, [(i, i ^ 1) for i in range(count)])  145 us
    all_to_all x4, waiting for transfers between devices, exchange(): lax.all_to_all(block, 'expert', split_axis=0, concat_axis=0, tiled=True,...  121 us
    all_to_all x4, starting transfers between devices, exchange(): lax.all_to_all(block, 'expert', split_axis=0, concat_axis=0, tiled=True,...  37.5 us
    dot_general x2, matrix products, per_device(): lax.dot_general(pre_grad, up, against_rows, preferred_element_type=f32)  20 us
    dot_general x2, matrix products, per_device(): product = jnp.dot(hidden, down, preferred_element_type=f32)  19.1 us
    ppermute x2, waiting for transfers between devices, shifted(): lax.ppermute(shard, axis, [(i, (i + by) % size) for i in range(size)])  11.2 us
    reshape x2, local copies, waits for them, and re-layouts, per_device(): part.astype(jnp.bfloat16).reshape(rows // 4, 4, model_width)  11.2 us
    dot_general x2, matrix products, per_device(): pre_act = jnp.dot(x_rows, up, preferred_element_type=f32)  9.09 us
  transfers between devices with their start and end apart: 8, of which 6 were waited for; matrix products, arithmetic and copies ran while one was open for 19% of the time, Pallas kernels for 4%

profile of v1, /device:TPU:24, one launch (start us, length us, event | category | flops | bytes accessed | tf_op | source)
XLA Modules:
  0.0 420.3 jit_solution(13200107705242000105)
XLA Ops:
  0.6 4.0 dispatch_fwd.1
  4.6 12.2 %all-to-all-start = ((bf16[96,4,3584]{2,1,0:T(4,128)(2,1)}), bf16[96,4,3584]{2,1,0:T(4,128)(2,1)S(1)}, u32[]{:S(2)}, u32[]{:S(2)}) async-start(bf16[96,4,3584]{2,1,0:T(4,128)(2,1)} %dispatch_fwd.1), calls=%async_computation | async-start | bytes 5505024 | tf_op jit(solution)/shard_map/all_to_all | solution.py:135
  16.8 7.4 %dispatch_bwd.1 = bf16[768,3584]{1,0:T(8,128)(2,1)} custom-call(s32[2,128]{1,0:T(2,128)} %bitcast.56, bf16[128,3584]{1,0:T(8,128)(2,1)} %bitcast.51, bf16[128,3584]{1,0:T(8,128)(2,1)} %bitcast.49), custom_call_target="tpu_custom_call" | custom-call | tf_op jit(solution)/shard_map/dispatch_bwd/pallas_call | solution.py:148
  24.2 55.5 %all-to-all-done = bf16[96,4,3584]{2,1,0:T(4,128)(2,1)S(1)} async-done(((bf16[96,4,3584]{2,1,0:T(4,128)(2,1)}), bf16[96,4,3584]{2,1,0:T(4,128)(2,1)S(1)}, u32[]{:S(2)}, u32[]{:S(2)}) %all-to-all-start) | async-done | bytes 2752544 | tf_op jit(solution)/shard_map/all_to_all | solution.py:135
  79.7 7.4 %all-to-all-start.2 = ((bf16[32,24,3584]{2,1,0:T(8,128)(2,1)}), bf16[32,24,3584]{2,1,0:T(8,128)(2,1)}, u32[]{:S(2)}, u32[]{:S(2)}) async-start(bf16[32,24,3584]{2,1,0:T(8,128)(2,1)} %bitcast.46), calls=%async_computation.2 | async-start | bytes 11010048 | tf_op jit(solution)/shard_map/all_to_all | solution.py:135
  87.1 0.1 collective-permute-start
  87.2 2.0 collective-permute-start.1
  89.2 2.3 reshape.23
  91.5 0.0 copy-start.1
  91.5 9.6 %fusion.13 = f32[384,3584]{1,0:T(8,128)} fusion(bf16[1,512,3584]{2,1,0:T(8,128)(2,1)} %param.17, bf16[384,3584]{1,0:T(8,128)(2,1)} %reshape.23, bf16[1,3584,512]{2,1,0:T(8,128)(2,1)} %param.16), kind=kOutput, calls=%fused_computation.19 | convolution fusion | flops 2819555328 | bytes 15597568 | tf_op jit(solution)/shard_map/dot_general | solution.py:165
  101.1 68.6 %collective-permute-done = bf16[3584,512]{1,0:T(8,128)(2,1)} collective-permute-done((bf16[3584,512]{1,0:T(8,128)(2,1)}, bf16[3584,512]{1,0:T(8,128)(2,1)}, u32[]{:S(2)}, u32[]{:S(2)}) %collective-permute-start) | collective-permute-done | bytes 3670048 | tf_op jit(solution)/shard_map/ppermute | solution.py:20
  169.7 76.9 %collective-permute-done.1 = bf16[512,3584]{1,0:T(8,128)(2,1)} collective-permute-done((bf16[512,3584]{1,0:T(8,128)(2,1)}, bf16[512,3584]{1,0:T(8,128)(2,1)}, u32[]{:S(2)}, u32[]{:S(2)}) %collective-permute-start.1) | collective-permute-done | bytes 3670048 | tf_op jit(solution)/shard_map/ppermute | solution.py:20
  246.6 0.0 copy-done.1
  246.6 9.5 %fusion = bf16[384,3584]{1,0:T(8,128)(2,1)} fusion(f32[384,3584]{1,0:T(8,128)} %fusion.13, bf16[512,3584]{1,0:T(8,128)(2,1)} %collective-permute-done.1, bf16[384,3584]{1,0:T(8,128)(2,1)S(1)} %copy-done.1, bf16[3584,512]{1,0:T(8,128)(2,1)} %collective-permute-done), kind=kOutput, calls=%fused_computation.2 | convolution fusion | flops 2822307840 | bytes 18350080 | tf_op jit(solution)/shard_map/dot_general | solution.py:165
  256.1 5.6 %reshape.24 = bf16[96,4,3584]{2,1,0:T(4,128)(2,1)} reshape(bf16[384,3584]{1,0:T(8,128)(2,1)} %fusion) | data formatting | bytes 5505024 | tf_op jit(solution)/shard_map/reshape | solution.py:167
  261.7 0.0 all-to-all-done.2
  261.7 10.4 %all-to-all-start.1 = ((bf16[96,4,3584]{2,1,0:T(4,128)(2,1)}), bf16[96,4,3584]{2,1,0:T(4,128)(2,1)S(1)}, u32[]{:S(2)}, u32[]{:S(2)}) async-start(bf16[96,4,3584]{2,1,0:T(4,128)(2,1)} %reshape.24), calls=%async_computation.1 | async-start | bytes 5505024 | tf_op jit(solution)/shard_map/all_to_all | solution.py:135
  272.1 7.2 %fusion.34 = (bf16[32,12,3584]{2,1,0:T(8,128)(2,1)}, bf16[32,12,3584]{2,1,0:T(8,128)(2,1)}) fusion(bf16[32,24,3584]{2,1,0:T(8,128)(2,1)} %all-to-all-done.2), kind=kLoop, calls=%fused_computation.35 | loop fusion | bytes 11010048 | tf_op jit(solution)/shard_map/slice | solution.py:170
  279.3 5.4 %reshape.26 = bf16[384,3584]{1,0:T(8,128)(2,1)} reshape(bf16[32,12,3584]{2,1,0:T(8,128)(2,1)} %get-tuple-element.2) | data formatting | bytes 5505024 | tf_op jit(solution)/shard_map/reshape | solution.py:170
  284.7 5.4 %reshape.25 = bf16[384,3584]{1,0:T(8,128)(2,1)} reshape(bf16[32,12,3584]{2,1,0:T(8,128)(2,1)} %get-tuple-element.3) | data formatting | bytes 5505024 | tf_op jit(solution)/shard_map/reshape | solution.py:171
  290.0 0.0 copy-start.2
  290.0 5.5 %fusion.22 = f32[384,512]{1,0:T(8,128)} fusion(bf16[384,3584]{1,0:T(8,128)(2,1)} %reshape.26, bf16[1,3584,512]{2,1,0:T(8,128)(2,1)} %param.16), kind=kOutput, calls=%fused_computation.27 | convolution fusion | flops 1409286144 | bytes 7208960 | tf_op jit(solution)/shard_map/dot_general | solution.py:174
  295.5 0.0 copy-done.2
  295.5 3.6 fusion.37
  299.1 9.8 %fusion.4 = f32[384,3584]{1,0:T(8,128)} fusion(bf16[384,3584]{1,0:T(8,128)(2,1)} %reshape.25, f32[384,512]{1,0:T(8,128)} %fusion.22, bf16[1,512,3584]{2,1,0:T(8,128)(2,1)} %param.17, bf16[1,3584,512]{2,1,0:T(8,128)(2,1)} %param.16), kind=kOutput, calls=%fused_computation.8 | convolution fusion | flops 2820341760 | bytes 16384000 | tf_op jit(solution)/shard_map/dot_general | solution.py:177
  308.9 10.3 %fusion.1 = bf16[384,3584]{1,0:T(8,128)(2,1)} fusion(f32[384,3584]{1,0:T(8,128)} %fusion.4, bf16[3584,512]{1,0:T(8,128)(2,1)} %collective-permute-done, bf16[384,3584]{1,0:T(8,128)(2,1)} %reshape.25, bf16[512,3584]{1,0:T(8,128)(2,1)} %collective-permute-done.1, f32[384,512]{1,0:T(8,128)S(1)} %fusion.37), kind=kOutput, calls=%fused_computation.3 | convolution fusion | flops 2823094272 | bytes 19136512 | tf_op jit(solution)/shard_map/dot_general | solution.py:177
  319.1 5.6 %reshape.27 = bf16[96,4,3584]{2,1,0:T(4,128)(2,1)} reshape(bf16[384,3584]{1,0:T(8,128)(2,1)} %fusion.1) | data formatting | bytes 5505024 | tf_op jit(solution)/shard_map/reshape | solution.py:179
  324.7 8.7 %all-to-all-done.1.back_ref = bf16[96,4,3584]{2,1,0:T(4,128)(2,1)S(1)} async-done(((bf16[96,4,3584]{2,1,0:T(4,128)(2,1)}), bf16[96,4,3584]{2,1,0:T(4,128)(2,1)S(1)}, u32[]{:S(2)}, u32[]{:S(2)}) %all-to-all-start.1) | async-done | bytes 2752544 | tf_op jit(solution)/shard_map/all_to_all | solution.py:135
  333.4 0.0 copy-start
  333.4 7.5 %all-to-all-start.3 = ((bf16[96,4,3584]{2,1,0:T(4,128)(2,1)}), bf16[96,4,3584]{2,1,0:T(4,128)(2,1)}, u32[]{:S(2)}, u32[]{:S(2)}) async-start(bf16[96,4,3584]{2,1,0:T(4,128)(2,1)} %reshape.27), calls=%async_computation.3 | async-start | bytes 5505024 | tf_op jit(solution)/shard_map/all_to_all | solution.py:135
  340.9 0.0 copy-done
  340.9 4.5 %combine_fwd.1 = bf16[128,3584]{1,0:T(8,128)(2,1)} custom-call(s32[2,128]{1,0:T(2,128)} %bitcast.55, f32[2,128]{1,0:T(2,128)} %bitcast.58, bf16[128,3584]{1,0:T(8,128)(2,1)} %bitcast.48, bf16[96,4,3584]{2,1,0:T(4,128)(2,1)} %copy-done), custom_call_target="tpu_custom_call" | custom-call | tf_op jit(solution)/shard_map/combine_fwd/pallas_call | solution.py:182
  345.5 0.0 collective-permute-start.2
  345.5 57.2 %all-to-all-done.3.back_ref = bf16[96,4,3584]{2,1,0:T(4,128)(2,1)} async-done(((bf16[96,4,3584]{2,1,0:T(4,128)(2,1)}), bf16[96,4,3584]{2,1,0:T(4,128)(2,1)}, u32[]{:S(2)}, u32[]{:S(2)}) %all-to-all-start.3) | async-done | bytes 2752544 | tf_op jit(solution)/shard_map/all_to_all | solution.py:135
  402.7 4.5 %combine_bwd.1 = bf16[128,3584]{1,0:T(8,128)(2,1)} custom-call(s32[2,128]{1,0:T(2,128)} %bitcast.57, f32[2,128]{1,0:T(2,128)} %bitcast.59, bf16[128,3584]{1,0:T(8,128)(2,1)} %bitcast.50, bf16[96,4,3584]{2,1,0:T(4,128)(2,1)} %all-to-all-done.3.back_ref), custom_call_target="tpu_custom_call" | custom-call | tf_op jit(solution)/shard_map/combine_bwd/pallas_call | solution.py:182
  407.2 0.0 collective-permute-start.3
  407.2 0.0 collective-permute-done.2
  407.2 11.2 %collective-permute-done.3 = bf16[1,128,3584]{2,1,0:T(8,128)(2,1)S(1)} collective-permute-done((bf16[1,128,3584]{2,1,0:T(8,128)(2,1)}, bf16[1,128,3584]{2,1,0:T(8,128)(2,1)S(1)}, u32[]{:S(2)}, u32[]{:S(2)}) %collective-permute-start.3) | collective-permute-done | bytes 917536 | tf_op jit(solution)/shard_map/ppermute | solution.py:25
  418.4 0.9 copy.13
  419.4 0.9 copy.14
Async XLA Ops:
  4.6 75.1 %all-to-all-start = ((bf16[96,4,3584]{2,1,0:T(4,128)(2,1)}), bf16[96,4,3584]{2,1,0:T(4,128)(2,1)S(1)}, u32[]{:S(2)}, u32[]{:S(2)}) async-start(bf16[96,4,3584]{2,1,0:T(4,128)(2,1)} %dispatch_fwd.1), calls=%async_computation | async-start | bytes 5505024 | tf_op jit(solution)/shard_map/all_to_all | solution.py:135
  79.7 182.0 %all-to-all-start.2 = ((bf16[32,24,3584]{2,1,0:T(8,128)(2,1)}), bf16[32,24,3584]{2,1,0:T(8,128)(2,1)}, u32[]{:S(2)}, u32[]{:S(2)}) async-start(bf16[32,24,3584]{2,1,0:T(8,128)(2,1)} %bitcast.46), calls=%async_computation.2 | async-start | bytes 11010048 | tf_op jit(solution)/shard_map/all_to_all | solution.py:135
  87.1 82.6 %collective-permute-start = (bf16[3584,512]{1,0:T(8,128)(2,1)}, bf16[3584,512]{1,0:T(8,128)(2,1)}, u32[]{:S(2)}, u32[]{:S(2)}) collective-permute-start(bf16[3584,512]{1,0:T(8,128)(2,1)} %bitcast.61), channel_id=1, source_target_pairs={{0,1},{1,0},{2,3},{3,2},{4,5},{5,4},{6,7},{7,6},{8,9},{9,8},{10,11... | collective-permute-start | bytes 11010056 | tf_op jit(solution)/shard_map/ppermute | solution.py:20
  87.2 159.4 %collective-permute-start.1 = (bf16[512,3584]{1,0:T(8,128)(2,1)}, bf16[512,3584]{1,0:T(8,128)(2,1)}, u32[]{:S(2)}, u32[]{:S(2)}) collective-permute-start(bf16[512,3584]{1,0:T(8,128)(2,1)} %bitcast.60), channel_id=1, source_target_pairs={{0,1},{1,0},{2,3},{3,2},{4,5},{5,4},{6,7},{7,6},{8,9},{9,8},{10,11... | collective-permute-start | bytes 11010056 | tf_op jit(solution)/shard_map/ppermute | solution.py:20
  91.5 155.1 %copy-start.1 = (bf16[384,3584]{1,0:T(8,128)(2,1)S(1)}, bf16[384,3584]{1,0:T(8,128)(2,1)}, u32[]{:S(2)}) copy-start(bf16[384,3584]{1,0:T(8,128)(2,1)} %reshape.23) | copy-start | bytes 8257540
  261.7 71.8 %all-to-all-start.1 = ((bf16[96,4,3584]{2,1,0:T(4,128)(2,1)}), bf16[96,4,3584]{2,1,0:T(4,128)(2,1)S(1)}, u32[]{:S(2)}, u32[]{:S(2)}) async-start(bf16[96,4,3584]{2,1,0:T(4,128)(2,1)} %reshape.24), calls=%async_computation.1 | async-start | bytes 5505024 | tf_op jit(solution)/shard_map/all_to_all | solution.py:135
  290.0 5.5 %copy-start.2 = (bf16[384,3584]{1,0:T(8,128)(2,1)S(1)}, bf16[384,3584]{1,0:T(8,128)(2,1)}, u32[]{:S(2)}) copy-start(bf16[384,3584]{1,0:T(8,128)(2,1)} %reshape.26) | copy-start | bytes 8257540
  333.4 7.5 %copy-start = (bf16[96,4,3584]{2,1,0:T(4,128)(2,1)}, bf16[96,4,3584]{2,1,0:T(4,128)(2,1)S(1)}, u32[]{:S(2)}) copy-start(bf16[96,4,3584]{2,1,0:T(4,128)(2,1)S(1)} %all-to-all-done.1.back_ref) | copy-start | bytes 8257540
  333.4 69.2 %all-to-all-start.3 = ((bf16[96,4,3584]{2,1,0:T(4,128)(2,1)}), bf16[96,4,3584]{2,1,0:T(4,128)(2,1)}, u32[]{:S(2)}, u32[]{:S(2)}) async-start(bf16[96,4,3584]{2,1,0:T(4,128)(2,1)} %reshape.27), calls=%async_computation.3 | async-start | bytes 5505024 | tf_op jit(solution)/shard_map/all_to_all | solution.py:135
  345.5 61.7 %collective-permute-start.2 = (bf16[1,128,3584]{2,1,0:T(8,128)(2,1)}, bf16[1,128,3584]{2,1,0:T(8,128)(2,1)S(1)}, u32[]{:S(2)}, u32[]{:S(2)}) collective-permute-start(bf16[1,128,3584]{2,1,0:T(8,128)(2,1)} %bitcast.52), channel_id=1, source_target_pairs={{0,64},{64,128},{128,192},{192,0},{1,65},{65,129},{129,193},{193,1... | collective-permute-start | bytes 2752520 | tf_op jit(solution)/shard_map/ppermute | solution.py:25
  407.2 11.2 %collective-permute-start.3 = (bf16[1,128,3584]{2,1,0:T(8,128)(2,1)}, bf16[1,128,3584]{2,1,0:T(8,128)(2,1)S(1)}, u32[]{:S(2)}, u32[]{:S(2)}) collective-permute-start(bf16[1,128,3584]{2,1,0:T(8,128)(2,1)} %bitcast.53), channel_id=1, source_target_pairs={{0,192},{64,0},{128,64},{192,128},{1,193},{65,1},{129,65},{193,129... | collective-permute-start | bytes 2752520 | tf_op jit(solution)/shard_map/ppermute | solution.py:25

commit v2 on v1

--- a/solution.py
+++ b/solution.py
@@ -6,6 +6,7 @@
 from jax.experimental import pallas as pl
 from jax.experimental.pallas import tpu as pltpu
 from jax.sharding import PartitionSpec as P
+
 
 VMEM = pl.BlockSpec(memory_space=pltpu.VMEM)
 
@@ -47,7 +48,7 @@
 
 
 def slot_rows(place, block, first, capacity):
-    experts, tokens = place.shape
+    experts, _ = place.shape
     rows = experts * block
     row = lax.broadcasted_iota(jnp.int32, (rows, experts), 0)
     col = lax.broadcasted_iota(jnp.int32, (rows, experts), 1)
@@ -102,7 +103,7 @@
     out_ref[...] = total.astype(jnp.bfloat16)
 
 
-def per_device(
+def layer(
     x_fwd,
     routes_fwd,
     affinity_fwd,
@@ -178,19 +179,18 @@
         part = product if part is None else part + product
     back_b = exchange(part.astype(jnp.bfloat16).reshape(rows // 4, 4, model_width))
 
-    def combine(routes, affinity, x, back, name):
+    def combine(routes, affinity, x, back):
         return pl.pallas_call(
             functools.partial(combine_kernel, capacity, experts),
             out_shape=jax.ShapeDtypeStruct((tokens, model_width), jnp.bfloat16),
             in_specs=[VMEM] * 4,
             out_specs=VMEM,
             compiler_params=params,
-            name=name,
         )(routes, affinity, x, back)
 
-    layer_out = combine(routes_f, affinity_fwd[0].T, x_fwd[0], back_f, "combine_fwd")
+    layer_out = combine(routes_f, affinity_fwd[0].T, x_fwd[0], back_f)
     fwd_next = shifted(layer_out[None], "section", 1)
-    input_grad = combine(routes_b, affinity_bwd[0].T, grad_bwd[0], back_b, "combine_bwd")
+    input_grad = combine(routes_b, affinity_bwd[0].T, grad_bwd[0], back_b)
     bwd_next = shifted(input_grad[None], "section", -1)
     return (fwd_next, bwd_next)
 
@@ -199,5 +199,5 @@
     rows = P("section", "expert", None)
     in_specs = (rows,) * 7 + (P("section", None, "expert"), rows)
     return jax.shard_map(
-        per_device, mesh=mesh, in_specs=in_specs, out_specs=(rows, rows), check_vma=False
+        layer, mesh=mesh, in_specs=in_specs, out_specs=(rows, rows), check_vma=False
     )

time: 428 us -> 428 us (level)
  no operation moved by 1% of the time
where the time goes in v2:
time: 428 us; the launch traced here: 420 us
  waiting for transfers between devices  278 us (65%)
  matrix products  48.2 us (11%)
  starting transfers between devices  39.6 us (9%)
  local copies, waits for them, and re-layouts  33.3 us (8%)
  Pallas kernels  20.4 us (5%)
    ppermute x2, waiting for transfers between devices, from_partner(): return lax.ppermute(block, axis, [(i, i ^ 1) for i in range(count)])  145 us
    all_to_all x4, waiting for transfers between devices, exchange(): lax.all_to_all(block, 'expert', split_axis=0, concat_axis=0, tiled=True,...  121 us
    all_to_all x4, starting transfers between devices, exchange(): lax.all_to_all(block, 'expert', split_axis=0, concat_axis=0, tiled=True,...  37.5 us
    dot_general x2, matrix products, layer(): lax.dot_general(pre_grad, up, against_rows, preferred_element_type=f32)  20 us
    dot_general x2, matrix products, layer(): product = jnp.dot(hidden, down, preferred_element_type=f32)  19.1 us
    ppermute x2, waiting for transfers between devices, shifted(): lax.ppermute(shard, axis, [(i, (i + by) % size) for i in range(size)])  11.2 us
    reshape x2, local copies, waits for them, and re-layouts, layer(): part.astype(jnp.bfloat16).reshape(rows // 4, 4, model_width)  11.2 us
    dot_general x2, matrix products, layer(): pre_act = jnp.dot(x_rows, up, preferred_element_type=f32)  9.09 us
  transfers between devices with their start and end apart: 8, of which 6 were waited for; matrix products, arithmetic and copies ran while one was open for 19% of the time, Pallas kernels for 4%

profile of v2, /device:TPU:24, one launch (start us, length us, event | category | flops | bytes accessed | tf_op | source)
XLA Modules:
  0.0 420.3 jit_solution(13200107705242000105)
XLA Ops:
  0.6 4.0 dispatch_fwd.1
  4.6 12.2 %all-to-all-start = ((bf16[96,4,3584]{2,1,0:T(4,128)(2,1)}), bf16[96,4,3584]{2,1,0:T(4,128)(2,1)S(1)}, u32[]{:S(2)}, u32[]{:S(2)}) async-start(bf16[96,4,3584]{2,1,0:T(4,128)(2,1)} %dispatch_fwd.1), calls=%async_computation | async-start | bytes 5505024 | tf_op jit(solution)/shard_map/all_to_all | solution.py:136
  16.8 7.4 %dispatch_bwd.1 = bf16[768,3584]{1,0:T(8,128)(2,1)} custom-call(s32[2,128]{1,0:T(2,128)} %bitcast.56, bf16[128,3584]{1,0:T(8,128)(2,1)} %bitcast.51, bf16[128,3584]{1,0:T(8,128)(2,1)} %bitcast.49), custom_call_target="tpu_custom_call" | custom-call | tf_op jit(solution)/shard_map/dispatch_bwd/pallas_call | solution.py:149
  24.2 55.5 %all-to-all-done = bf16[96,4,3584]{2,1,0:T(4,128)(2,1)S(1)} async-done(((bf16[96,4,3584]{2,1,0:T(4,128)(2,1)}), bf16[96,4,3584]{2,1,0:T(4,128)(2,1)S(1)}, u32[]{:S(2)}, u32[]{:S(2)}) %all-to-all-start) | async-done | bytes 2752544 | tf_op jit(solution)/shard_map/all_to_all | solution.py:136
  79.7 7.4 %all-to-all-start.2 = ((bf16[32,24,3584]{2,1,0:T(8,128)(2,1)}), bf16[32,24,3584]{2,1,0:T(8,128)(2,1)}, u32[]{:S(2)}, u32[]{:S(2)}) async-start(bf16[32,24,3584]{2,1,0:T(8,128)(2,1)} %bitcast.46), calls=%async_computation.2 | async-start | bytes 11010048 | tf_op jit(solution)/shard_map/all_to_all | solution.py:136
  87.1 0.1 collective-permute-start
  87.2 2.0 collective-permute-start.1
  89.2 2.3 reshape.23
  91.5 0.0 copy-start.1
  91.5 9.6 %fusion.13 = f32[384,3584]{1,0:T(8,128)} fusion(bf16[1,512,3584]{2,1,0:T(8,128)(2,1)} %param.17, bf16[384,3584]{1,0:T(8,128)(2,1)} %reshape.23, bf16[1,3584,512]{2,1,0:T(8,128)(2,1)} %param.16), kind=kOutput, calls=%fused_computation.19 | convolution fusion | flops 2819555328 | bytes 15597568 | tf_op jit(solution)/shard_map/dot_general | solution.py:166
  101.1 68.6 %collective-permute-done = bf16[3584,512]{1,0:T(8,128)(2,1)} collective-permute-done((bf16[3584,512]{1,0:T(8,128)(2,1)}, bf16[3584,512]{1,0:T(8,128)(2,1)}, u32[]{:S(2)}, u32[]{:S(2)}) %collective-permute-start) | collective-permute-done | bytes 3670048 | tf_op jit(solution)/shard_map/ppermute | solution.py:21
  169.7 76.9 %collective-permute-done.1 = bf16[512,3584]{1,0:T(8,128)(2,1)} collective-permute-done((bf16[512,3584]{1,0:T(8,128)(2,1)}, bf16[512,3584]{1,0:T(8,128)(2,1)}, u32[]{:S(2)}, u32[]{:S(2)}) %collective-permute-start.1) | collective-permute-done | bytes 3670048 | tf_op jit(solution)/shard_map/ppermute | solution.py:21
  246.6 0.0 copy-done.1
  246.6 9.5 %fusion = bf16[384,3584]{1,0:T(8,128)(2,1)} fusion(f32[384,3584]{1,0:T(8,128)} %fusion.13, bf16[512,3584]{1,0:T(8,128)(2,1)} %collective-permute-done.1, bf16[384,3584]{1,0:T(8,128)(2,1)S(1)} %copy-done.1, bf16[3584,512]{1,0:T(8,128)(2,1)} %collective-permute-done), kind=kOutput, calls=%fused_computation.2 | convolution fusion | flops 2822307840 | bytes 18350080 | tf_op jit(solution)/shard_map/dot_general | solution.py:166
  256.1 5.6 %reshape.24 = bf16[96,4,3584]{2,1,0:T(4,128)(2,1)} reshape(bf16[384,3584]{1,0:T(8,128)(2,1)} %fusion) | data formatting | bytes 5505024 | tf_op jit(solution)/shard_map/reshape | solution.py:168
  261.7 0.0 all-to-all-done.2
  261.7 10.4 %all-to-all-start.1 = ((bf16[96,4,3584]{2,1,0:T(4,128)(2,1)}), bf16[96,4,3584]{2,1,0:T(4,128)(2,1)S(1)}, u32[]{:S(2)}, u32[]{:S(2)}) async-start(bf16[96,4,3584]{2,1,0:T(4,128)(2,1)} %reshape.24), calls=%async_computation.1 | async-start | bytes 5505024 | tf_op jit(solution)/shard_map/all_to_all | solution.py:136
  272.1 7.2 %fusion.34 = (bf16[32,12,3584]{2,1,0:T(8,128)(2,1)}, bf16[32,12,3584]{2,1,0:T(8,128)(2,1)}) fusion(bf16[32,24,3584]{2,1,0:T(8,128)(2,1)} %all-to-all-done.2), kind=kLoop, calls=%fused_computation.35 | loop fusion | bytes 11010048 | tf_op jit(solution)/shard_map/slice | solution.py:171
  279.3 5.4 %reshape.26 = bf16[384,3584]{1,0:T(8,128)(2,1)} reshape(bf16[32,12,3584]{2,1,0:T(8,128)(2,1)} %get-tuple-element.2) | data formatting | bytes 5505024 | tf_op jit(solution)/shard_map/reshape | solution.py:171
  284.7 5.4 %reshape.25 = bf16[384,3584]{1,0:T(8,128)(2,1)} reshape(bf16[32,12,3584]{2,1,0:T(8,128)(2,1)} %get-tuple-element.3) | data formatting | bytes 5505024 | tf_op jit(solution)/shard_map/reshape | solution.py:172
  290.0 0.0 copy-start.2
  290.0 5.5 %fusion.22 = f32[384,512]{1,0:T(8,128)} fusion(bf16[384,3584]{1,0:T(8,128)(2,1)} %reshape.26, bf16[1,3584,512]{2,1,0:T(8,128)(2,1)} %param.16), kind=kOutput, calls=%fused_computation.27 | convolution fusion | flops 1409286144 | bytes 7208960 | tf_op jit(solution)/shard_map/dot_general | solution.py:175
  295.5 0.0 copy-done.2
  295.5 3.6 fusion.37
  299.1 9.8 %fusion.4 = f32[384,3584]{1,0:T(8,128)} fusion(bf16[384,3584]{1,0:T(8,128)(2,1)} %reshape.25, f32[384,512]{1,0:T(8,128)} %fusion.22, bf16[1,512,3584]{2,1,0:T(8,128)(2,1)} %param.17, bf16[1,3584,512]{2,1,0:T(8,128)(2,1)} %param.16), kind=kOutput, calls=%fused_computation.8 | convolution fusion | flops 2820341760 | bytes 16384000 | tf_op jit(solution)/shard_map/dot_general | solution.py:178
  308.9 10.3 %fusion.1 = bf16[384,3584]{1,0:T(8,128)(2,1)} fusion(f32[384,3584]{1,0:T(8,128)} %fusion.4, bf16[3584,512]{1,0:T(8,128)(2,1)} %collective-permute-done, bf16[384,3584]{1,0:T(8,128)(2,1)} %reshape.25, bf16[512,3584]{1,0:T(8,128)(2,1)} %collective-permute-done.1, f32[384,512]{1,0:T(8,128)S(1)} %fusion.37), kind=kOutput, calls=%fused_computation.3 | convolution fusion | flops 2823094272 | bytes 19136512 | tf_op jit(solution)/shard_map/dot_general | solution.py:178
  319.1 5.6 %reshape.27 = bf16[96,4,3584]{2,1,0:T(4,128)(2,1)} reshape(bf16[384,3584]{1,0:T(8,128)(2,1)} %fusion.1) | data formatting | bytes 5505024 | tf_op jit(solution)/shard_map/reshape | solution.py:180
  324.7 8.7 %all-to-all-done.1.back_ref = bf16[96,4,3584]{2,1,0:T(4,128)(2,1)S(1)} async-done(((bf16[96,4,3584]{2,1,0:T(4,128)(2,1)}), bf16[96,4,3584]{2,1,0:T(4,128)(2,1)S(1)}, u32[]{:S(2)}, u32[]{:S(2)}) %all-to-all-start.1) | async-done | bytes 2752544 | tf_op jit(solution)/shard_map/all_to_all | solution.py:136
  333.4 0.0 copy-start
  333.4 7.5 %all-to-all-start.3 = ((bf16[96,4,3584]{2,1,0:T(4,128)(2,1)}), bf16[96,4,3584]{2,1,0:T(4,128)(2,1)}, u32[]{:S(2)}, u32[]{:S(2)}) async-start(bf16[96,4,3584]{2,1,0:T(4,128)(2,1)} %reshape.27), calls=%async_computation.3 | async-start | bytes 5505024 | tf_op jit(solution)/shard_map/all_to_all | solution.py:136
  340.9 0.0 copy-done
  340.9 4.5 %shard_map.104 = bf16[128,3584]{1,0:T(8,128)(2,1)} custom-call(s32[2,128]{1,0:T(2,128)} %bitcast.55, f32[2,128]{1,0:T(2,128)} %bitcast.58, bf16[128,3584]{1,0:T(8,128)(2,1)} %bitcast.48, bf16[96,4,3584]{2,1,0:T(4,128)(2,1)} %copy-done), custom_call_target="tpu_custom_call" | custom-call | tf_op jit(solution)/shard_map/pallas_call | solution.py:183
  345.5 0.0 collective-permute-start.2
  345.5 57.2 %all-to-all-done.3.back_ref = bf16[96,4,3584]{2,1,0:T(4,128)(2,1)} async-done(((bf16[96,4,3584]{2,1,0:T(4,128)(2,1)}), bf16[96,4,3584]{2,1,0:T(4,128)(2,1)}, u32[]{:S(2)}, u32[]{:S(2)}) %all-to-all-start.3) | async-done | bytes 2752544 | tf_op jit(solution)/shard_map/all_to_all | solution.py:136
  402.7 4.5 %shard_map.105 = bf16[128,3584]{1,0:T(8,128)(2,1)} custom-call(s32[2,128]{1,0:T(2,128)} %bitcast.57, f32[2,128]{1,0:T(2,128)} %bitcast.59, bf16[128,3584]{1,0:T(8,128)(2,1)} %bitcast.50, bf16[96,4,3584]{2,1,0:T(4,128)(2,1)} %all-to-all-done.3.back_ref), custom_call_target="tpu_custom_call" | custom-call | tf_op jit(solution)/shard_map/pallas_call | solution.py:183
  407.2 0.0 collective-permute-start.3
  407.2 0.0 collective-permute-done.2
  407.2 11.2 %collective-permute-done.3 = bf16[1,128,3584]{2,1,0:T(8,128)(2,1)S(1)} collective-permute-done((bf16[1,128,3584]{2,1,0:T(8,128)(2,1)}, bf16[1,128,3584]{2,1,0:T(8,128)(2,1)S(1)}, u32[]{:S(2)}, u32[]{:S(2)}) %collective-permute-start.3) | collective-permute-done | bytes 917536 | tf_op jit(solution)/shard_map/ppermute | solution.py:26
  418.4 0.9 copy.13
  419.4 0.9 copy.14
Async XLA Ops:
  4.6 75.1 %all-to-all-start = ((bf16[96,4,3584]{2,1,0:T(4,128)(2,1)}), bf16[96,4,3584]{2,1,0:T(4,128)(2,1)S(1)}, u32[]{:S(2)}, u32[]{:S(2)}) async-start(bf16[96,4,3584]{2,1,0:T(4,128)(2,1)} %dispatch_fwd.1), calls=%async_computation | async-start | bytes 5505024 | tf_op jit(solution)/shard_map/all_to_all | solution.py:136
  79.7 182.0 %all-to-all-start.2 = ((bf16[32,24,3584]{2,1,0:T(8,128)(2,1)}), bf16[32,24,3584]{2,1,0:T(8,128)(2,1)}, u32[]{:S(2)}, u32[]{:S(2)}) async-start(bf16[32,24,3584]{2,1,0:T(8,128)(2,1)} %bitcast.46), calls=%async_computation.2 | async-start | bytes 11010048 | tf_op jit(solution)/shard_map/all_to_all | solution.py:136
  87.1 82.6 %collective-permute-start = (bf16[3584,512]{1,0:T(8,128)(2,1)}, bf16[3584,512]{1,0:T(8,128)(2,1)}, u32[]{:S(2)}, u32[]{:S(2)}) collective-permute-start(bf16[3584,512]{1,0:T(8,128)(2,1)} %bitcast.61), channel_id=1, source_target_pairs={{0,1},{1,0},{2,3},{3,2},{4,5},{5,4},{6,7},{7,6},{8,9},{9,8},{10,11... | collective-permute-start | bytes 11010056 | tf_op jit(solution)/shard_map/ppermute | solution.py:21
  87.2 159.4 %collective-permute-start.1 = (bf16[512,3584]{1,0:T(8,128)(2,1)}, bf16[512,3584]{1,0:T(8,128)(2,1)}, u32[]{:S(2)}, u32[]{:S(2)}) collective-permute-start(bf16[512,3584]{1,0:T(8,128)(2,1)} %bitcast.60), channel_id=1, source_target_pairs={{0,1},{1,0},{2,3},{3,2},{4,5},{5,4},{6,7},{7,6},{8,9},{9,8},{10,11... | collective-permute-start | bytes 11010056 | tf_op jit(solution)/shard_map/ppermute | solution.py:21
  91.5 155.1 %copy-start.1 = (bf16[384,3584]{1,0:T(8,128)(2,1)S(1)}, bf16[384,3584]{1,0:T(8,128)(2,1)}, u32[]{:S(2)}) copy-start(bf16[384,3584]{1,0:T(8,128)(2,1)} %reshape.23) | copy-start | bytes 8257540
  261.7 71.8 %all-to-all-start.1 = ((bf16[96,4,3584]{2,1,0:T(4,128)(2,1)}), bf16[96,4,3584]{2,1,0:T(4,128)(2,1)S(1)}, u32[]{:S(2)}, u32[]{:S(2)}) async-start(bf16[96,4,3584]{2,1,0:T(4,128)(2,1)} %reshape.24), calls=%async_computation.1 | async-start | bytes 5505024 | tf_op jit(solution)/shard_map/all_to_all | solution.py:136
  290.0 5.5 %copy-start.2 = (bf16[384,3584]{1,0:T(8,128)(2,1)S(1)}, bf16[384,3584]{1,0:T(8,128)(2,1)}, u32[]{:S(2)}) copy-start(bf16[384,3584]{1,0:T(8,128)(2,1)} %reshape.26) | copy-start | bytes 8257540
  333.4 7.5 %copy-start = (bf16[96,4,3584]{2,1,0:T(4,128)(2,1)}, bf16[96,4,3584]{2,1,0:T(4,128)(2,1)S(1)}, u32[]{:S(2)}) copy-start(bf16[96,4,3584]{2,1,0:T(4,128)(2,1)S(1)} %all-to-all-done.1.back_ref) | copy-start | bytes 8257540
  333.4 69.2 %all-to-all-start.3 = ((bf16[96,4,3584]{2,1,0:T(4,128)(2,1)}), bf16[96,4,3584]{2,1,0:T(4,128)(2,1)}, u32[]{:S(2)}, u32[]{:S(2)}) async-start(bf16[96,4,3584]{2,1,0:T(4,128)(2,1)} %reshape.27), calls=%async_computation.3 | async-start | bytes 5505024 | tf_op jit(solution)/shard_map/all_to_all | solution.py:136
  345.5 61.7 %collective-permute-start.2 = (bf16[1,128,3584]{2,1,0:T(8,128)(2,1)}, bf16[1,128,3584]{2,1,0:T(8,128)(2,1)S(1)}, u32[]{:S(2)}, u32[]{:S(2)}) collective-permute-start(bf16[1,128,3584]{2,1,0:T(8,128)(2,1)} %bitcast.52), channel_id=1, source_target_pairs={{0,64},{64,128},{128,192},{192,0},{1,65},{65,129},{129,193},{193,1... | collective-permute-start | bytes 2752520 | tf_op jit(solution)/shard_map/ppermute | solution.py:26
  407.2 11.2 %collective-permute-start.3 = (bf16[1,128,3584]{2,1,0:T(8,128)(2,1)}, bf16[1,128,3584]{2,1,0:T(8,128)(2,1)S(1)}, u32[]{:S(2)}, u32[]{:S(2)}) collective-permute-start(bf16[1,128,3584]{2,1,0:T(8,128)(2,1)} %bitcast.53), channel_id=1, source_target_pairs={{0,192},{64,0},{128,64},{192,128},{1,193},{65,1},{129,65},{193,129... | collective-permute-start | bytes 2752520 | tf_op jit(solution)/shard_map/ppermute | solution.py:26

commit v3 on v2

--- a/solution.py
+++ b/solution.py
@@ -9,6 +9,9 @@
 
 
 VMEM = pl.BlockSpec(memory_space=pltpu.VMEM)
+ANY = pl.BlockSpec(memory_space=pl.ANY)
+AGAINST_ROWS = (((1,), (1,)), ((), ()))
+STEP = 512
 
 
 def same_side_groups(devices):
@@ -79,12 +82,76 @@
     pick_g = as_bf16(slot_rows(place, 2 * capacity, capacity, capacity))
     rows = jnp.dot(pick_x, x_ref[...], preferred_element_type=jnp.float32)
     rows = rows + jnp.dot(pick_g, g_ref[...], preferred_element_type=jnp.float32)
-    out_ref[...] = rows.astype(jnp.bfloat16)
-
-
-def combine_kernel(capacity, experts, routes_ref, affinity_ref, x_ref, back_ref, out_ref):
-    routes = routes_ref[...]
-    affinity = affinity_ref[...]
+    out_ref[...] = rows.reshape(out_ref.shape).astype(jnp.bfloat16)
+
+
+def start_loads(up_own, down_own, up_other, down_other, ups, downs, sems):
+    pairs = ((up_own, ups.at[0]), (down_own, downs.at[0]), (up_other, ups.at[1]), (down_other, downs.at[1]))
+    loads = [pltpu.make_async_copy(src, dst, sems.at[i]) for i, (src, dst) in enumerate(pairs)]
+    for load in loads:
+        load.start()
+    return loads
+
+
+def expert_fwd_kernel(
+    recv_ref, up_own, down_own, up_other, down_other, out_ref, ups, downs, hidden, sems
+):
+    groups, per_group, width = out_ref.shape
+    rows = groups * per_group
+    half = hidden.shape[1] // 2
+    loads = start_loads(up_own, down_own, up_other, down_other, ups, downs, sems)
+    x = recv_ref[...].reshape(rows, width)
+    for i in range(2):
+        loads[2 * i].wait()
+        pre_act = jnp.dot(x, ups[i], preferred_element_type=jnp.float32)
+        hidden[:, i * half : (i + 1) * half] = jax.nn.silu(pre_act).astype(jnp.bfloat16)
+    loads[1].wait()
+    loads[3].wait()
+    for c in range(0, width, STEP):
+        part = jnp.dot(
+            hidden[:, :half], downs[0, :, c : c + STEP], preferred_element_type=jnp.float32
+        )
+        part = part + jnp.dot(
+            hidden[:, half:], downs[1, :, c : c + STEP], preferred_element_type=jnp.float32
+        )
+        out_ref[:, :, c : c + STEP] = part.reshape(groups, per_group, STEP).astype(jnp.bfloat16)
+
+
+def expert_bwd_kernel(
+    recv_ref, up_own, down_own, up_other, down_other, out_ref, ups, downs, hidden, sems
+):
+    groups, per_group, width = out_ref.shape
+    rows = groups * per_group
+    half = hidden.shape[1] // 2
+    loads = start_loads(up_own, down_own, up_other, down_other, ups, downs, sems)
+    sources = hidden.shape[1] // 32
+    both = recv_ref[...].reshape(sources, 2 * groups // sources, per_group, width)
+    x = both[:, : groups // sources].reshape(rows, width)
+    g = both[:, groups // sources :].reshape(rows, width)
+    for i in range(2):
+        loads[2 * i].wait()
+        pre_act = jnp.dot(x, ups[i], preferred_element_type=jnp.float32)
+        loads[2 * i + 1].wait()
+        hidden_grad = lax.dot_general(
+            g, downs[i], AGAINST_ROWS, preferred_element_type=jnp.float32
+        )
+        pre_grad = hidden_grad * silu_grad(pre_act)
+        hidden[:, i * half : (i + 1) * half] = pre_grad.astype(jnp.bfloat16)
+    for c in range(0, width, STEP):
+        part = lax.dot_general(
+            hidden[:, :half], ups[0, c : c + STEP, :], AGAINST_ROWS,
+            preferred_element_type=jnp.float32,
+        )
+        part = part + lax.dot_general(
+            hidden[:, half:], ups[1, c : c + STEP, :], AGAINST_ROWS,
+            preferred_element_type=jnp.float32,
+        )
+        out_ref[:, :, c : c + STEP] = part.reshape(groups, per_group, STEP).astype(jnp.bfloat16)
+
+
+def combine_kernel(capacity, experts, info_ref, x_ref, back_ref, out_ref):
+    routes = info_ref[0:2, :].astype(jnp.int32)
+    affinity = info_ref[2:4, :]
     tokens = routes.shape[1]
     rows = experts * capacity
     pick = slot_rows(place_of(routes, experts), capacity, 0, capacity)
@@ -148,7 +215,7 @@
     recv_f = exchange(send_f)
     send_b = pl.pallas_call(
         functools.partial(dispatch_bwd_kernel, capacity, experts),
-        out_shape=jax.ShapeDtypeStruct((2 * rows, model_width), jnp.bfloat16),
+        out_shape=jax.ShapeDtypeStruct((rows // 2, 4, model_width), jnp.bfloat16),
         in_specs=[VMEM] * 3,
         out_specs=VMEM,
         compiler_params=params,
@@ -156,43 +223,50 @@
     )(routes_b, x_bwd[0], grad_bwd[0])
     recv_b = exchange(send_b)
 
-    f32 = jnp.float32
-    against_rows = (((1,), (1,)), ((), ()))
-
-    x_rows = recv_f.reshape(rows, model_width)
-    part = None
-    for up, down in ((up_own, down_own), (up_other, down_other)):
-        hidden = jax.nn.silu(jnp.dot(x_rows, up, preferred_element_type=f32)).astype(jnp.bfloat16)
-        product = jnp.dot(hidden, down, preferred_element_type=f32)
-        part = product if part is None else part + product
-    back_f = exchange(part.astype(jnp.bfloat16).reshape(rows // 4, 4, model_width))
-
-    blocks = recv_b.reshape(experts, 2 * capacity, model_width)
-    x_rows = blocks[:, :capacity].reshape(rows, model_width)
-    g_rows = blocks[:, capacity:].reshape(rows, model_width)
-    part = None
-    for up, down in ((up_own, down_own), (up_other, down_other)):
-        pre_act = jnp.dot(x_rows, up, preferred_element_type=f32)
-        hidden_grad = lax.dot_general(g_rows, down, against_rows, preferred_element_type=f32)
-        pre_grad = (hidden_grad * silu_grad(pre_act)).astype(jnp.bfloat16)
-        product = lax.dot_general(pre_grad, up, against_rows, preferred_element_type=f32)
-        part = product if part is None else part + product
-    back_b = exchange(part.astype(jnp.bfloat16).reshape(rows // 4, 4, model_width))
-
-    def combine(routes, affinity, x, back):
+    half = up_own.shape[1]
+
+    def serve(kernel, received):
+        return pl.pallas_call(
+            kernel,
+            out_shape=jax.ShapeDtypeStruct((rows // 4, 4, model_width), jnp.bfloat16),
+            in_specs=[VMEM] + [ANY] * 4,
+            out_specs=VMEM,
+            scratch_shapes=[
+                pltpu.VMEM((2, model_width, half), jnp.bfloat16),
+                pltpu.VMEM((2, half, model_width), jnp.bfloat16),
+                pltpu.VMEM((rows, 2 * half), jnp.bfloat16),
+                pltpu.SemaphoreType.DMA((4,)),
+            ],
+            compiler_params=params,
+        )(received, up_own, down_own, up_other, down_other)
+
+    def combine(info, x, back):
         return pl.pallas_call(
             functools.partial(combine_kernel, capacity, experts),
             out_shape=jax.ShapeDtypeStruct((tokens, model_width), jnp.bfloat16),
-            in_specs=[VMEM] * 4,
+            in_specs=[VMEM] * 3,
             out_specs=VMEM,
             compiler_params=params,
-        )(routes, affinity, x, back)
-
-    layer_out = combine(routes_f, affinity_fwd[0].T, x_fwd[0], back_f)
-    fwd_next = shifted(layer_out[None], "section", 1)
-    input_grad = combine(routes_b, affinity_bwd[0].T, grad_bwd[0], back_b)
-    bwd_next = shifted(input_grad[None], "section", -1)
-    return (fwd_next, bwd_next)
+        )(info, x, back)
+
+    def info_of(routes, affinity):
+        return jnp.concatenate([routes.astype(jnp.float32), affinity[0].T], 0)
+
+    x_f = shifted(x_fwd[0], "section", 1)
+    x_b = shifted(grad_bwd[0], "section", -1)
+    info_f = shifted(info_of(routes_f, affinity_fwd), "section", 1)
+    info_b = shifted(info_of(routes_b, affinity_bwd), "section", -1)
+
+    served_f = serve(expert_fwd_kernel, recv_f)
+    served_f = shifted(served_f, "section", 1)
+    back_f = exchange(served_f)
+    served_b = serve(expert_bwd_kernel, recv_b)
+    served_b = shifted(served_b, "section", -1)
+    back_b = exchange(served_b)
+
+    fwd_next = combine(info_f, x_f, back_f)
+    bwd_next = combine(info_b, x_b, back_b)
+    return (fwd_next[None], bwd_next[None])
 
 
 def solution(mesh):

time: 428 us -> 454 us (1.061)
  waiting for transfers between devices: 278 us -> 344 us
  matrix products: 48.2 us -> 0 us
  Pallas kernels: 20.4 us -> 48.9 us
  local copies, waits for them, and re-layouts: 33.3 us -> 6.13 us
  starting transfers between devices: 39.6 us -> 48.8 us
    ppermute x2 -> x6, waiting for transfers between devices: 11.2 us -> 121 us  [shifted(): lax.ppermute(shard, axis, [(i, (i + by) % size) for i in range(size)])]
    all_to_all x4, waiting for transfers between devices: 121 us -> 65.5 us  [exchange(): lax.all_to_all(block, 'expert', split_axis=0, concat_axis=0, tiled=True,...]
    dot_general x6 -> x0, matrix products: 48.2 us -> none  [the longest x2 20 us: layer(): lax.dot_general(pre_grad, up, against_rows, preferred_element_type=f32)]
    pallas_call x0 -> x2, Pallas kernels: none -> 27.9 us  [serve(): pl.pallas_call(kernel, out_shape=jax.ShapeDtypeStruct((rows // 4, 4, mode...]
    reshape x5 -> x0, local copies, waits for them, and re-layouts: 24.3 us -> none  [the longest x2 11.2 us: layer(): part.astype(jnp.bfloat16).reshape(rows // 4, 4, model_width)]
    ppermute x2, waiting for transfers between devices: 145 us -> 157 us  [from_partner(): return lax.ppermute(block, axis, [(i, i ^ 1) for i in range(count)])]
    ppermute x2 -> x6, starting transfers between devices: 0.01 us -> 7.56 us  [shifted(): lax.ppermute(shard, axis, [(i, (i + by) % size) for i in range(size)])]
    slice x1 -> x0, local copies, waits for them, and re-layouts: 7.16 us -> none  [layer(): x_rows = blocks[:, :capacity].reshape(rows, model_width)]
  transfers between devices with their start and end apart: 8 -> 12, of which waited for: 6 -> 7; matrix products, arithmetic and copies ran while one was open for 19% -> 0% of each run, Pallas kernels for 4% -> 9%
where the time goes in v3:
time: 454 us; the launch traced here: 449 us
  waiting for transfers between devices  344 us (76%)
  Pallas kernels  48.9 us (11%)
  starting transfers between devices  48.8 us (11%)
  local copies, waits for them, and re-layouts  6.13 us (1%)
    ppermute x2, waiting for transfers between devices, from_partner(): return lax.ppermute(block, axis, [(i, i ^ 1) for i in range(count)])  157 us
    ppermute x6, waiting for transfers between devices, shifted(): lax.ppermute(shard, axis, [(i, (i + by) % size) for i in range(size)])  121 us
    all_to_all x4, waiting for transfers between devices, exchange(): lax.all_to_all(block, 'expert', split_axis=0, concat_axis=0, tiled=True,...  65.5 us
    all_to_all x4, starting transfers between devices, exchange(): lax.all_to_all(block, 'expert', split_axis=0, concat_axis=0, tiled=True,...  39.1 us
    pallas_call x2, Pallas kernels, serve(): pl.pallas_call(kernel, out_shape=jax.ShapeDtypeStruct((rows // 4, 4, mode...  27.9 us
  transfers between devices with their start and end apart: 12, of which 7 were waited for; matrix products, arithmetic and copies ran while one was open for 0% of the time, Pallas kernels for 9%

profile of v3, /device:TPU:24, one launch (start us, length us, event | category | flops | bytes accessed | tf_op | source)
XLA Modules:
  0.0 448.7 jit_solution(12119863165087881619)
XLA Ops:
  0.6 4.0 dispatch_fwd.1
  4.7 12.2 %all-to-all-start = ((bf16[96,4,3584]{2,1,0:T(4,128)(2,1)}), bf16[96,4,3584]{2,1,0:T(4,128)(2,1)S(1)}, u32[]{:S(2)}, u32[]{:S(2)}) async-start(bf16[96,4,3584]{2,1,0:T(4,128)(2,1)} %dispatch_fwd.1), calls=%async_computation | async-start | bytes 5505024 | tf_op jit(solution)/shard_map/all_to_all | solution.py:203
  16.9 8.0 %dispatch_bwd.1 = bf16[192,4,3584]{2,1,0:T(4,128)(2,1)} custom-call(s32[2,128]{1,0:T(2,128)} %bitcast.35, bf16[128,3584]{1,0:T(8,128)(2,1)} %bitcast.27, bf16[128,3584]{1,0:T(8,128)(2,1)} %bitcast.30), custom_call_target="tpu_custom_call" | custom-call | tf_op jit(solution)/shard_map/dispatch_bwd/pallas_call | solution.py:216
  24.8 54.9 %all-to-all-done.recv_ref = bf16[96,4,3584]{2,1,0:T(4,128)(2,1)S(1)} async-done(((bf16[96,4,3584]{2,1,0:T(4,128)(2,1)}), bf16[96,4,3584]{2,1,0:T(4,128)(2,1)S(1)}, u32[]{:S(2)}, u32[]{:S(2)}) %all-to-all-start) | async-done | bytes 2752544 | tf_op jit(solution)/shard_map/all_to_all | solution.py:203
  79.7 0.0 copy-start.1
  79.7 1.5 copy-done.1
  81.3 7.4 %all-to-all-start.2 = ((bf16[192,4,3584]{2,1,0:T(4,128)(2,1)}), bf16[192,4,3584]{2,1,0:T(4,128)(2,1)}, u32[]{:S(2)}, u32[]{:S(2)}) async-start(bf16[192,4,3584]{2,1,0:T(4,128)(2,1)} %dispatch_bwd.1), calls=%async_computation.2 | async-start | bytes 11010048 | tf_op jit(solution)/shard_map/all_to_all | solution.py:203
  88.7 0.1 collective-permute-start.2
  88.8 2.0 collective-permute-start.3
  90.8 80.4 %collective-permute-done.2.up_other = bf16[3584,512]{1,0:T(8,128)(2,1)S(1)} collective-permute-done((bf16[3584,512]{1,0:T(8,128)(2,1)}, bf16[3584,512]{1,0:T(8,128)(2,1)S(1)}, u32[]{:S(2)}, u32[]{:S(2)}) %collective-permute-start.2) | collective-permute-done | bytes 3670048 | tf_op jit(solution)/shard_map/ppermute | solution.py:24
  171.2 77.0 %collective-permute-done.3.down_other = bf16[512,3584]{1,0:T(8,128)(2,1)} collective-permute-done((bf16[512,3584]{1,0:T(8,128)(2,1)}, bf16[512,3584]{1,0:T(8,128)(2,1)}, u32[]{:S(2)}, u32[]{:S(2)}) %collective-permute-start.3) | collective-permute-done | bytes 3670048 | tf_op jit(solution)/shard_map/ppermute | solution.py:24
  248.1 0.0 copy-done
  248.1 12.2 %shard_map.104 = bf16[96,4,3584]{2,1,0:T(4,128)(2,1)} custom-call(bf16[96,4,3584]{2,1,0:T(4,128)(2,1)} %copy-done.1, bf16[3584,512]{1,0:T(8,128)(2,1)} %bitcast.22, bf16[512,3584]{1,0:T(8,128)(2,1)} %bitcast.25, bf16[3584,512]{1,0:T(8,128)(2,1)} %copy-done, bf16[512,3584]{1,0:T(8,128)(2,1)} %collective-permute-done.3.down_other), custom_call_target="tpu_custom_call" | custom-call | tf_op jit(solution)/shard_map/pallas_call | solution.py:229
  260.4 0.3 collective-permute-start.4
  260.6 34.2 %collective-permute-done.4 = bf16[96,4,3584]{2,1,0:T(4,128)(2,1)S(1)} collective-permute-done((bf16[96,4,3584]{2,1,0:T(4,128)(2,1)}, bf16[96,4,3584]{2,1,0:T(4,128)(2,1)S(1)}, u32[]{:S(2)}, u32[]{:S(2)}) %collective-permute-start.4) | collective-permute-done | bytes 2752544 | tf_op jit(solution)/shard_map/ppermute | solution.py:29
  294.8 1.5 copy-done.3
  296.3 0.0 all-to-all-done.2.recv_ref
  296.3 10.4 %all-to-all-start.1 = ((bf16[96,4,3584]{2,1,0:T(4,128)(2,1)}), bf16[96,4,3584]{2,1,0:T(4,128)(2,1)S(1)}, u32[]{:S(2)}, u32[]{:S(2)}) async-start(bf16[96,4,3584]{2,1,0:T(4,128)(2,1)} %copy-done.3), calls=%async_computation.1 | async-start | bytes 5505024 | tf_op jit(solution)/shard_map/all_to_all | solution.py:203
  306.8 15.7 %shard_map.106 = bf16[96,4,3584]{2,1,0:T(4,128)(2,1)} custom-call(bf16[192,4,3584]{2,1,0:T(4,128)(2,1)} %all-to-all-done.2.recv_ref, bf16[3584,512]{1,0:T(8,128)(2,1)} %bitcast.23, bf16[512,3584]{1,0:T(8,128)(2,1)} %bitcast.26, bf16[3584,512]{1,0:T(8,128)(2,1)} %copy-done, bf16[512,3584]{1,0:T(8,128)(2,1)} %collective-permute-done.3.down_other), custom_call_target="tpu_custom_call" | custom-call | tf_op jit(solution)/shard_map/pallas_call | solution.py:229
  322.4 0.0 copy-start.6
  322.4 0.0 copy-start.10
  322.4 0.0 copy-start.7
  322.5 0.0 copy-start.11
  322.5 0.1 collective-permute-start.7
  322.6 48.6 %collective-permute-done.7 = bf16[96,4,3584]{2,1,0:T(4,128)(2,1)} collective-permute-done((bf16[96,4,3584]{2,1,0:T(4,128)(2,1)}, bf16[96,4,3584]{2,1,0:T(4,128)(2,1)}, u32[]{:S(2)}, u32[]{:S(2)}) %collective-permute-start.7) | collective-permute-done | bytes 2752544 | tf_op jit(solution)/shard_map/ppermute | solution.py:29
  371.1 0.0 all-to-all-done.1.back_ref
  371.1 1.6 copy-done.2
  372.7 9.1 %all-to-all-start.3 = ((bf16[96,4,3584]{2,1,0:T(4,128)(2,1)}), bf16[96,4,3584]{2,1,0:T(4,128)(2,1)}, u32[]{:S(2)}, u32[]{:S(2)}) async-start(bf16[96,4,3584]{2,1,0:T(4,128)(2,1)} %collective-permute-done.7), calls=%async_computation.3 | async-start | bytes 5505024 | tf_op jit(solution)/shard_map/all_to_all | solution.py:203
  381.8 1.7 collective-permute-start.1
  383.5 1.9 collective-permute-start.6
  385.4 0.0 copy-done.6
  385.4 0.0 copy-done.10
  385.4 0.1 collective-permute-start
  385.5 0.0 copy-done.7
  385.6 0.0 copy-done.11
  385.6 3.5 collective-permute-start.5
  389.1 38.4 %collective-permute-done.info_ref = f32[4,128]{1,0:T(4,128)S(1)} collective-permute-done((f32[4,128]{1,0:T(4,128)S(1)}, f32[4,128]{1,0:T(4,128)S(1)}, u32[]{:S(2)}, u32[]{:S(2)}) %collective-permute-start) | collective-permute-done | bytes 2080 | tf_op jit(solution)/shard_map/ppermute | solution.py:29
  427.5 0.0 collective-permute-done.1.x_ref
  427.5 0.6 copy-done.9
  428.1 0.9 copy-done.5
  429.0 4.5 %shard_map.105 = bf16[128,3584]{1,0:T(8,128)(2,1)} custom-call(f32[4,128]{1,0:T(4,128)} %copy-done.9, bf16[128,3584]{1,0:T(8,128)(2,1)} %copy-done.5, bf16[96,4,3584]{2,1,0:T(4,128)(2,1)} %copy-done.2), custom_call_target="tpu_custom_call" | custom-call | tf_op jit(solution)/shard_map/pallas_call | solution.py:244
  433.5 0.0 collective-permute-done.5.info_ref
  433.5 0.0 collective-permute-done.6.x_ref
  433.5 0.0 copy-start.4
  433.5 10.6 %all-to-all-done.3.back_ref = bf16[96,4,3584]{2,1,0:T(4,128)(2,1)} async-done(((bf16[96,4,3584]{2,1,0:T(4,128)(2,1)}), bf16[96,4,3584]{2,1,0:T(4,128)(2,1)}, u32[]{:S(2)}, u32[]{:S(2)}) %all-to-all-start.3) | async-done | bytes 2752544 | tf_op jit(solution)/shard_map/all_to_all | solution.py:203
  444.2 0.0 copy-done.8
  444.2 0.0 copy-done.4
  444.2 4.5 %shard_map.107 = bf16[128,3584]{1,0:T(8,128)(2,1)} custom-call(f32[4,128]{1,0:T(4,128)} %copy-done.8, bf16[128,3584]{1,0:T(8,128)(2,1)} %copy-done.4, bf16[96,4,3584]{2,1,0:T(4,128)(2,1)} %all-to-all-done.3.back_ref), custom_call_target="tpu_custom_call" | custom-call | tf_op jit(solution)/shard_map/pallas_call | solution.py:244
  (10 shorter events, 0.0 us)
Async XLA Ops:
  4.7 75.1 %all-to-all-start = ((bf16[96,4,3584]{2,1,0:T(4,128)(2,1)}), bf16[96,4,3584]{2,1,0:T(4,128)(2,1)S(1)}, u32[]{:S(2)}, u32[]{:S(2)}) async-start(bf16[96,4,3584]{2,1,0:T(4,128)(2,1)} %dispatch_fwd.1), calls=%async_computation | async-start | bytes 5505024 | tf_op jit(solution)/shard_map/all_to_all | solution.py:203
  79.7 1.5 copy-start.1
  81.3 215.1 %all-to-all-start.2 = ((bf16[192,4,3584]{2,1,0:T(4,128)(2,1)}), bf16[192,4,3584]{2,1,0:T(4,128)(2,1)}, u32[]{:S(2)}, u32[]{:S(2)}) async-start(bf16[192,4,3584]{2,1,0:T(4,128)(2,1)} %dispatch_bwd.1), calls=%async_computation.2 | async-start | bytes 11010048 | tf_op jit(solution)/shard_map/all_to_all | solution.py:203
  88.7 82.5 %collective-permute-start.2 = (bf16[3584,512]{1,0:T(8,128)(2,1)}, bf16[3584,512]{1,0:T(8,128)(2,1)S(1)}, u32[]{:S(2)}, u32[]{:S(2)}) collective-permute-start(bf16[3584,512]{1,0:T(8,128)(2,1)} %bitcast.21), channel_id=1, source_target_pairs={{0,1},{1,0},{2,3},{3,2},{4,5},{5,4},{6,7},{7,6},{8,9},{9,8},{10,11... | collective-permute-start | bytes 11010056 | tf_op jit(solution)/shard_map/ppermute | solution.py:24
  88.8 159.4 %collective-permute-start.3 = (bf16[512,3584]{1,0:T(8,128)(2,1)}, bf16[512,3584]{1,0:T(8,128)(2,1)}, u32[]{:S(2)}, u32[]{:S(2)}) collective-permute-start(bf16[512,3584]{1,0:T(8,128)(2,1)} %bitcast.24), channel_id=1, source_target_pairs={{0,1},{1,0},{2,3},{3,2},{4,5},{5,4},{6,7},{7,6},{8,9},{9,8},{10,11... | collective-permute-start | bytes 11010056 | tf_op jit(solution)/shard_map/ppermute | solution.py:24
  171.2 77.0 %copy-start = (bf16[3584,512]{1,0:T(8,128)(2,1)}, bf16[3584,512]{1,0:T(8,128)(2,1)S(1)}, u32[]{:S(2)}) copy-start(bf16[3584,512]{1,0:T(8,128)(2,1)S(1)} %collective-permute-done.2.up_other) | copy-start | bytes 11010052
  260.4 34.5 %collective-permute-start.4 = (bf16[96,4,3584]{2,1,0:T(4,128)(2,1)}, bf16[96,4,3584]{2,1,0:T(4,128)(2,1)S(1)}, u32[]{:S(2)}, u32[]{:S(2)}) collective-permute-start(bf16[96,4,3584]{2,1,0:T(4,128)(2,1)} %shard_map.104), channel_id=1, source_target_pairs={{0,64},{64,128},{128,192},{192,0},{1,65},{65,129},{129,193},{193,1... | collective-permute-start | bytes 8257544 | tf_op jit(solution)/shard_map/ppermute | solution.py:29
  294.8 1.5 copy-start.3
  296.3 74.8 %all-to-all-start.1 = ((bf16[96,4,3584]{2,1,0:T(4,128)(2,1)}), bf16[96,4,3584]{2,1,0:T(4,128)(2,1)S(1)}, u32[]{:S(2)}, u32[]{:S(2)}) async-start(bf16[96,4,3584]{2,1,0:T(4,128)(2,1)} %copy-done.3), calls=%async_computation.1 | async-start | bytes 5505024 | tf_op jit(solution)/shard_map/all_to_all | solution.py:203
  322.4 63.0 %copy-start.6 = (s32[1,128,2]{1,2,0:T(2,128)S(1)}, s32[1,128,2]{1,2,0:T(2,128)}, u32[]{:S(2)}) copy-start(s32[1,128,2]{1,2,0:T(2,128)} %param.10) | copy-start | bytes 3076
  322.4 63.0 %copy-start.10 = (f32[1,128,2]{1,2,0:T(2,128)S(1)}, f32[1,128,2]{1,2,0:T(2,128)}, u32[]{:S(2)}) copy-start(f32[1,128,2]{1,2,0:T(2,128)} %param.11) | copy-start | bytes 3076
  322.4 63.1 %copy-start.7 = (s32[1,128,2]{1,2,0:T(2,128)S(1)}, s32[1,128,2]{1,2,0:T(2,128)}, u32[]{:S(2)}) copy-start(s32[1,128,2]{1,2,0:T(2,128)} %param.14) | copy-start | bytes 3076
  322.5 63.1 %copy-start.11 = (f32[1,128,2]{1,2,0:T(2,128)S(1)}, f32[1,128,2]{1,2,0:T(2,128)}, u32[]{:S(2)}) copy-start(f32[1,128,2]{1,2,0:T(2,128)} %param.15) | copy-start | bytes 3076
  322.5 48.6 %collective-permute-start.7 = (bf16[96,4,3584]{2,1,0:T(4,128)(2,1)}, bf16[96,4,3584]{2,1,0:T(4,128)(2,1)}, u32[]{:S(2)}, u32[]{:S(2)}) collective-permute-start(bf16[96,4,3584]{2,1,0:T(4,128)(2,1)} %shard_map.106), channel_id=1, source_target_pairs={{0,192},{64,0},{128,64},{192,128},{1,193},{65,1},{129,65},{193,129... | collective-permute-start | bytes 8257544 | tf_op jit(solution)/shard_map/ppermute | solution.py:29
  371.1 1.6 copy-start.2
  372.7 71.5 %all-to-all-start.3 = ((bf16[96,4,3584]{2,1,0:T(4,128)(2,1)}), bf16[96,4,3584]{2,1,0:T(4,128)(2,1)}, u32[]{:S(2)}, u32[]{:S(2)}) async-start(bf16[96,4,3584]{2,1,0:T(4,128)(2,1)} %collective-permute-done.7), calls=%async_computation.3 | async-start | bytes 5505024 | tf_op jit(solution)/shard_map/all_to_all | solution.py:203
  381.8 45.7 %collective-permute-start.1 = (bf16[128,3584]{1,0:T(8,128)(2,1)}, bf16[128,3584]{1,0:T(8,128)(2,1)S(1)}, u32[]{:S(2)}, u32[]{:S(2)}) collective-permute-start(bf16[128,3584]{1,0:T(8,128)(2,1)} %bitcast.29), channel_id=1, source_target_pairs={{0,64},{64,128},{128,192},{192,0},{1,65},{65,129},{129,193},{193,1... | collective-permute-start | bytes 2752520 | tf_op jit(solution)/shard_map/ppermute | solution.py:29
  383.5 50.0 %collective-permute-start.6 = (bf16[128,3584]{1,0:T(8,128)(2,1)}, bf16[128,3584]{1,0:T(8,128)(2,1)S(1)}, u32[]{:S(2)}, u32[]{:S(2)}) collective-permute-start(bf16[128,3584]{1,0:T(8,128)(2,1)} %bitcast.31), channel_id=1, source_target_pairs={{0,192},{64,0},{128,64},{192,128},{1,193},{65,1},{129,65},{193,129... | collective-permute-start | bytes 2752520 | tf_op jit(solution)/shard_map/ppermute | solution.py:29
  385.4 42.1 %collective-permute-start = (f32[4,128]{1,0:T(4,128)S(1)}, f32[4,128]{1,0:T(4,128)S(1)}, u32[]{:S(2)}, u32[]{:S(2)}) collective-permute-start(f32[4,128]{1,0:T(4,128)S(1)} %pad_maximum_fusion), channel_id=1, source_target_pairs={{0,64},{64,128},{128,192},{192,0},{1,65},{65,129},{129,193},{193,1... | collective-permute-start | bytes 6152 | tf_op jit(solution)/shard_map/ppermute | solution.py:29
  385.6 47.9 %collective-permute-start.5 = (f32[4,128]{1,0:T(4,128)S(1)}, f32[4,128]{1,0:T(4,128)S(1)}, u32[]{:S(2)}, u32[]{:S(2)}) collective-permute-start(f32[4,128]{1,0:T(4,128)S(1)} %pad_maximum_fusion.1), channel_id=1, source_target_pairs={{0,192},{64,0},{128,64},{192,128},{1,193},{65,1},{129,65},{193,129... | collective-permute-start | bytes 6152 | tf_op jit(solution)/shard_map/ppermute | solution.py:29
  427.5 0.6 copy-start.9
  428.1 0.9 copy-start.5
  433.5 10.6 %copy-start.8 = (f32[4,128]{1,0:T(4,128)}, f32[4,128]{1,0:T(4,128)S(1)}, u32[]{:S(2)}) copy-start(f32[4,128]{1,0:T(4,128)S(1)} %collective-permute-done.5.info_ref) | copy-start | bytes 6148
  433.5 10.6 %copy-start.4 = (bf16[128,3584]{1,0:T(8,128)(2,1)}, bf16[128,3584]{1,0:T(8,128)(2,1)S(1)}, u32[]{:S(2)}) copy-start(bf16[128,3584]{1,0:T(8,128)(2,1)S(1)} %collective-permute-done.6.x_ref) | copy-start | bytes 2752516

commit v4 on v3

--- a/solution.py
+++ b/solution.py
@@ -12,6 +12,7 @@
 ANY = pl.BlockSpec(memory_space=pl.ANY)
 AGAINST_ROWS = (((1,), (1,)), ((), ()))
 STEP = 512
+WIDE = 512
 
 
 def same_side_groups(devices):
@@ -69,20 +70,23 @@
     return mask.astype(jnp.float32).astype(jnp.bfloat16)
 
 
-def dispatch_fwd_kernel(capacity, experts, routes_ref, x_ref, out_ref):
-    place = place_of(routes_ref[...], experts)
-    pick = as_bf16(slot_rows(place, capacity, 0, capacity))
-    rows = jnp.dot(pick, x_ref[...], preferred_element_type=jnp.float32)
-    out_ref[...] = rows.reshape(out_ref.shape).astype(jnp.bfloat16)
-
-
-def dispatch_bwd_kernel(capacity, experts, routes_ref, x_ref, g_ref, out_ref):
-    place = place_of(routes_ref[...], experts)
-    pick_x = as_bf16(slot_rows(place, 2 * capacity, 0, capacity))
-    pick_g = as_bf16(slot_rows(place, 2 * capacity, capacity, capacity))
-    rows = jnp.dot(pick_x, x_ref[...], preferred_element_type=jnp.float32)
-    rows = rows + jnp.dot(pick_g, g_ref[...], preferred_element_type=jnp.float32)
-    out_ref[...] = rows.reshape(out_ref.shape).astype(jnp.bfloat16)
+def write_groups(out_ref, first, rows, members):
+    experts, groups = members, rows.shape[0] // members // 4
+    blocks = rows.reshape(experts, groups, 4, rows.shape[1])
+    out_ref[:, first : first + groups] = blocks.astype(jnp.bfloat16)
+
+
+def dispatch_kernel(capacity, experts, count, *refs):
+    routes_ref, x_refs, out_ref, pick_ref = refs[0], refs[1 : 1 + count], refs[-2], refs[-1]
+
+    @pl.when(pl.program_id(0) == 0)
+    def _():
+        place = place_of(routes_ref[...], experts)
+        pick_ref[...] = as_bf16(slot_rows(place, capacity, 0, capacity))
+
+    for i, x_ref in enumerate(x_refs):
+        rows = jnp.dot(pick_ref[...], x_ref[...], preferred_element_type=jnp.float32)
+        write_groups(out_ref, i * capacity // 4, rows, experts)
 
 
 def start_loads(up_own, down_own, up_other, down_other, ups, downs, sems):
@@ -149,24 +153,28 @@
         out_ref[:, :, c : c + STEP] = part.reshape(groups, per_group, STEP).astype(jnp.bfloat16)
 
 
-def combine_kernel(capacity, experts, info_ref, x_ref, back_ref, out_ref):
-    routes = info_ref[0:2, :].astype(jnp.int32)
-    affinity = info_ref[2:4, :]
-    tokens = routes.shape[1]
+def combine_kernel(capacity, experts, info_ref, x_ref, back_ref, out_ref, pick_ref, weight_ref):
+    tokens = x_ref.shape[0]
     rows = experts * capacity
-    pick = slot_rows(place_of(routes, experts), capacity, 0, capacity)
-    row = lax.broadcasted_iota(jnp.int32, (rows, tokens), 0)
-    weights = affinity / jnp.sum(affinity, 0, keepdims=True)
+
+    @pl.when(pl.program_id(0) == 0)
+    def _():
+        routes = info_ref[0:2, :].astype(jnp.int32)
+        affinity = info_ref[2:4, :]
+        pick = slot_rows(place_of(routes, experts), capacity, 0, capacity)
+        row = lax.broadcasted_iota(jnp.int32, (rows, tokens), 0)
+        weights = affinity / jnp.sum(affinity, 0, keepdims=True)
+        for k in range(2):
+            begin = routes[k : k + 1, :] * capacity
+            mine = pick & (row >= begin) & (row < begin + capacity)
+            pick_ref[k * tokens : (k + 1) * tokens, :] = as_bf16(mine).T
+            weight_ref[k] = jnp.broadcast_to(weights[k : k + 1, :], (tokens, tokens)).T
+
     back = back_ref[...].reshape(rows, x_ref.shape[1])
+    picked = jnp.dot(pick_ref[...], back, preferred_element_type=jnp.float32)
     total = x_ref[...].astype(jnp.float32)
     for k in range(2):
-        begin = routes[k : k + 1, :] * capacity
-        mine = pick & (row >= begin) & (row < begin + capacity)
-        picked = lax.dot_general(
-            as_bf16(mine), back, (((0,), (0,)), ((), ())), preferred_element_type=jnp.float32
-        )
-        weight = jnp.broadcast_to(weights[k : k + 1, :], (tokens, tokens)).T[:, 0:1]
-        total = total + weight * picked
+        total = total + weight_ref[k, :, 0:1] * picked[k * tokens : (k + 1) * tokens]
     out_ref[...] = total.astype(jnp.bfloat16)
 
 
@@ -204,24 +212,23 @@
             block, "expert", split_axis=0, concat_axis=0, tiled=True, axis_index_groups=groups
         )
 
-    send_f = pl.pallas_call(
-        functools.partial(dispatch_fwd_kernel, capacity, experts),
-        out_shape=jax.ShapeDtypeStruct((rows // 4, 4, model_width), jnp.bfloat16),
-        in_specs=[VMEM] * 2,
-        out_specs=VMEM,
-        compiler_params=params,
-        name="dispatch_fwd",
-    )(routes_f, x_fwd[0])
-    recv_f = exchange(send_f)
-    send_b = pl.pallas_call(
-        functools.partial(dispatch_bwd_kernel, capacity, experts),
-        out_shape=jax.ShapeDtypeStruct((rows // 2, 4, model_width), jnp.bfloat16),
-        in_specs=[VMEM] * 3,
-        out_specs=VMEM,
-        compiler_params=params,
-        name="dispatch_bwd",
-    )(routes_b, x_bwd[0], grad_bwd[0])
-    recv_b = exchange(send_b)
+    def dispatch(routes, blocks):
+        count = len(blocks)
+        groups_out = count * capacity // 4
+        sent = pl.pallas_call(
+            functools.partial(dispatch_kernel, capacity, experts, count),
+            grid=(model_width // WIDE,),
+            out_shape=jax.ShapeDtypeStruct((experts, groups_out, 4, model_width), jnp.bfloat16),
+            in_specs=[pl.BlockSpec((top_count, tokens), lambda i: (0, 0))]
+            + [pl.BlockSpec((tokens, WIDE), lambda i: (0, i))] * count,
+            out_specs=pl.BlockSpec((experts, groups_out, 4, WIDE), lambda i: (0, 0, 0, i)),
+            scratch_shapes=[pltpu.VMEM((rows, tokens), jnp.bfloat16)],
+            compiler_params=params,
+        )(routes, *blocks)
+        return sent.reshape(experts * groups_out, 4, model_width)
+
+    recv_b = exchange(dispatch(routes_b, (x_bwd[0], grad_bwd[0])))
+    recv_f = exchange(dispatch(routes_f, (x_fwd[0],)))
 
     half = up_own.shape[1]
 
@@ -243,30 +250,37 @@
     def combine(info, x, back):
         return pl.pallas_call(
             functools.partial(combine_kernel, capacity, experts),
+            grid=(model_width // WIDE,),
             out_shape=jax.ShapeDtypeStruct((tokens, model_width), jnp.bfloat16),
-            in_specs=[VMEM] * 3,
-            out_specs=VMEM,
+            in_specs=[
+                pl.BlockSpec((2 * top_count, tokens), lambda i: (0, 0)),
+                pl.BlockSpec((tokens, WIDE), lambda i: (0, i)),
+                pl.BlockSpec((rows // 4, 4, WIDE), lambda i: (0, 0, i)),
+            ],
+            out_specs=pl.BlockSpec((tokens, WIDE), lambda i: (0, i)),
+            scratch_shapes=[
+                pltpu.VMEM((top_count * tokens, rows), jnp.bfloat16),
+                pltpu.VMEM((top_count, tokens, tokens), jnp.float32),
+            ],
             compiler_params=params,
         )(info, x, back)
 
     def info_of(routes, affinity):
         return jnp.concatenate([routes.astype(jnp.float32), affinity[0].T], 0)
 
-    x_f = shifted(x_fwd[0], "section", 1)
-    x_b = shifted(grad_bwd[0], "section", -1)
-    info_f = shifted(info_of(routes_f, affinity_fwd), "section", 1)
-    info_b = shifted(info_of(routes_b, affinity_bwd), "section", -1)
-
+    served_b = serve(expert_bwd_kernel, recv_b)
+    back_b = exchange(served_b)
+
+    x_next = shifted(x_fwd[0], "section", 1)
+    info_next = shifted(info_of(routes_f, affinity_fwd), "section", 1)
     served_f = serve(expert_fwd_kernel, recv_f)
     served_f = shifted(served_f, "section", 1)
     back_f = exchange(served_f)
-    served_b = serve(expert_bwd_kernel, recv_b)
-    served_b = shifted(served_b, "section", -1)
-    back_b = exchange(served_b)
-
-    fwd_next = combine(info_f, x_f, back_f)
-    bwd_next = combine(info_b, x_b, back_b)
-    return (fwd_next[None], bwd_next[None])
+
+    input_grad = combine(info_of(routes_b, affinity_bwd), grad_bwd[0], back_b)
+    bwd_next = shifted(input_grad[None], "section", -1)
+    fwd_next = combine(info_next, x_next, back_f)
+    return (fwd_next[None], bwd_next)
 
 
 def solution(mesh):

time: 454 us -> 490 us (1.079)
  waiting for transfers between devices: 344 us -> 375 us
  Pallas kernels: 48.9 us -> 55.5 us
    all_to_all x4, waiting for transfers between devices: 65.5 us -> 137 us  [exchange(): lax.all_to_all(block, 'expert', split_axis=0, concat_axis=0, tiled=True,...]
    ppermute x6 -> x4, waiting for transfers between devices: 121 us -> 80.9 us  [shifted(): lax.ppermute(shard, axis, [(i, (i + by) % size) for i in range(size)])]
    pallas_call x4, Pallas kernels: 21 us -> 27.6 us  [the longest x2 13.9 us: dispatch(): pl.pallas_call(functools.partial(dispatch_kernel, capacity, experts, coun...]
  transfers between devices with their start and end apart: 12 -> 10, of which waited for: 7 -> 6; matrix products, arithmetic and copies ran while one was open for 0% -> 0% of each run, Pallas kernels for 9% -> 10%
where the time goes in v4:
time: 490 us; the launch traced here: 487 us
  waiting for transfers between devices  375 us (77%)
  Pallas kernels  55.5 us (11%)
  starting transfers between devices  49.6 us (10%)
  local copies, waits for them, and re-layouts  5.33 us (1%)
    ppermute x2, waiting for transfers between devices, from_partner(): return lax.ppermute(block, axis, [(i, i ^ 1) for i in range(count)])  157 us
    all_to_all x4, waiting for transfers between devices, exchange(): lax.all_to_all(block, 'expert', split_axis=0, concat_axis=0, tiled=True,...  137 us
    ppermute x4, waiting for transfers between devices, shifted(): lax.ppermute(shard, axis, [(i, (i + by) % size) for i in range(size)])  80.9 us
    all_to_all x4, starting transfers between devices, exchange(): lax.all_to_all(block, 'expert', split_axis=0, concat_axis=0, tiled=True,...  44 us
    pallas_call x2, Pallas kernels, serve(): pl.pallas_call(kernel, out_shape=jax.ShapeDtypeStruct((rows // 4, 4, mode...  27.8 us
    pallas_call x2, Pallas kernels, dispatch(): pl.pallas_call(functools.partial(dispatch_kernel, capacity, experts, coun...  13.9 us
    pallas_call x2, Pallas kernels, combine(): pl.pallas_call(functools.partial(combine_kernel, capacity, experts), grid...  13.7 us
  transfers between devices with their start and end apart: 10, of which 6 were waited for; matrix products, arithmetic and copies ran while one was open for 0% of the time, Pallas kernels for 10%

profile of v4, /device:TPU:24, one launch (start us, length us, event | category | flops | bytes accessed | tf_op | source)
XLA Modules:
  0.0 486.6 jit_solution(3340746660228077111)
XLA Ops:
  0.6 7.7 %shard_map.107 = bf16[32,6,4,3584]{3,2,1,0:T(4,128)(2,1)} custom-call(s32[2,128]{1,0:T(2,128)} %bitcast.39, bf16[128,3584]{1,0:T(8,128)(2,1)} %bitcast.33, bf16[128,3584]{1,0:T(8,128)(2,1)} %bitcast.31), custom_call_target="tpu_custom_call" | custom-call | tf_op jit(solution)/shard_map/pallas_call | solution.py:218
  8.3 12.3 %all-to-all-start.2 = ((bf16[192,4,3584]{2,1,0:T(4,128)(2,1)}), bf16[192,4,3584]{2,1,0:T(4,128)(2,1)}, u32[]{:S(2)}, u32[]{:S(2)}) async-start(bf16[192,4,3584]{2,1,0:T(4,128)(2,1)} %bitcast.23), calls=%async_computation.2 | async-start | bytes 11010048 | tf_op jit(solution)/shard_map/all_to_all | solution.py:211
  20.6 6.3 %shard_map.104 = bf16[32,3,4,3584]{3,2,1,0:T(4,128)(2,1)} custom-call(s32[2,128]{1,0:T(2,128)} %bitcast.38, bf16[128,3584]{1,0:T(8,128)(2,1)} %bitcast.34), custom_call_target="tpu_custom_call" | custom-call | tf_op jit(solution)/shard_map/pallas_call | solution.py:218
  26.8 115.6 %all-to-all-done.2.recv_ref = bf16[192,4,3584]{2,1,0:T(4,128)(2,1)} async-done(((bf16[192,4,3584]{2,1,0:T(4,128)(2,1)}), bf16[192,4,3584]{2,1,0:T(4,128)(2,1)}, u32[]{:S(2)}, u32[]{:S(2)}) %all-to-all-start.2) | async-done | bytes 5505056 | tf_op jit(solution)/shard_map/all_to_all | solution.py:211
  142.5 12.2 %all-to-all-start = ((bf16[96,4,3584]{2,1,0:T(4,128)(2,1)}), bf16[96,4,3584]{2,1,0:T(4,128)(2,1)}, u32[]{:S(2)}, u32[]{:S(2)}) async-start(bf16[96,4,3584]{2,1,0:T(4,128)(2,1)} %bitcast.30), calls=%async_computation | async-start | bytes 5505024 | tf_op jit(solution)/shard_map/all_to_all | solution.py:211
  154.7 0.1 collective-permute-start.2
  154.8 2.0 collective-permute-start.3
  156.8 80.4 %collective-permute-done.2.up_other = bf16[3584,512]{1,0:T(8,128)(2,1)S(1)} collective-permute-done((bf16[3584,512]{1,0:T(8,128)(2,1)}, bf16[3584,512]{1,0:T(8,128)(2,1)S(1)}, u32[]{:S(2)}, u32[]{:S(2)}) %collective-permute-start.2) | collective-permute-done | bytes 3670048 | tf_op jit(solution)/shard_map/ppermute | solution.py:25
  237.2 0.0 copy-start
  237.2 76.2 %collective-permute-done.3.down_other = bf16[512,3584]{1,0:T(8,128)(2,1)} collective-permute-done((bf16[512,3584]{1,0:T(8,128)(2,1)}, bf16[512,3584]{1,0:T(8,128)(2,1)}, u32[]{:S(2)}, u32[]{:S(2)}) %collective-permute-start.3) | collective-permute-done | bytes 3670048 | tf_op jit(solution)/shard_map/ppermute | solution.py:25
  313.3 0.0 copy-done
  313.3 15.6 %shard_map.108 = bf16[96,4,3584]{2,1,0:T(4,128)(2,1)} custom-call(bf16[192,4,3584]{2,1,0:T(4,128)(2,1)} %all-to-all-done.2.recv_ref, bf16[3584,512]{1,0:T(8,128)(2,1)} %bitcast.25, bf16[512,3584]{1,0:T(8,128)(2,1)} %bitcast.28, bf16[3584,512]{1,0:T(8,128)(2,1)} %copy-done, bf16[512,3584]{1,0:T(8,128)(2,1)} %collective-permute-done.3.down_other), custom_call_target="tpu_custom_call" | custom-call | tf_op jit(solution)/shard_map/pallas_call | solution.py:236
  328.9 0.0 all-to-all-done.recv_ref
  328.9 10.4 %all-to-all-start.3 = ((bf16[96,4,3584]{2,1,0:T(4,128)(2,1)}), bf16[96,4,3584]{2,1,0:T(4,128)(2,1)S(1)}, u32[]{:S(2)}, u32[]{:S(2)}) async-start(bf16[96,4,3584]{2,1,0:T(4,128)(2,1)} %shard_map.108), calls=%async_computation.3 | async-start | bytes 5505024 | tf_op jit(solution)/shard_map/all_to_all | solution.py:211
  339.4 12.3 %shard_map.105 = bf16[96,4,3584]{2,1,0:T(4,128)(2,1)} custom-call(bf16[96,4,3584]{2,1,0:T(4,128)(2,1)} %all-to-all-done.recv_ref, bf16[3584,512]{1,0:T(8,128)(2,1)} %bitcast.26, bf16[512,3584]{1,0:T(8,128)(2,1)} %bitcast.29, bf16[3584,512]{1,0:T(8,128)(2,1)} %copy-done, bf16[512,3584]{1,0:T(8,128)(2,1)} %collective-permute-done.3.down_other), custom_call_target="tpu_custom_call" | custom-call | tf_op jit(solution)/shard_map/pallas_call | solution.py:236
  351.6 0.0 copy-start.4
  351.7 0.0 copy-start.6
  351.7 0.1 collective-permute-start.4
  351.8 53.0 %collective-permute-done.4 = bf16[96,4,3584]{2,1,0:T(4,128)(2,1)} collective-permute-done((bf16[96,4,3584]{2,1,0:T(4,128)(2,1)}, bf16[96,4,3584]{2,1,0:T(4,128)(2,1)}, u32[]{:S(2)}, u32[]{:S(2)}) %collective-permute-start.4) | collective-permute-done | bytes 2752544 | tf_op jit(solution)/shard_map/ppermute | solution.py:30
  404.7 0.0 all-to-all-done.3.back_ref
  404.7 0.0 copy-start.2
  404.7 1.6 copy-done.2
  406.3 9.2 %all-to-all-start.1 = ((bf16[96,4,3584]{2,1,0:T(4,128)(2,1)}), bf16[96,4,3584]{2,1,0:T(4,128)(2,1)S(1)}, u32[]{:S(2)}, u32[]{:S(2)}) async-start(bf16[96,4,3584]{2,1,0:T(4,128)(2,1)} %collective-permute-done.4), calls=%async_computation.1 | async-start | bytes 5505024 | tf_op jit(solution)/shard_map/all_to_all | solution.py:211
  415.5 0.0 copy-start.3
  415.5 0.0 copy-start.7
  415.5 0.1 collective-permute-start.1
  415.6 0.0 copy-done.4
  415.6 0.0 copy-done.6
  415.6 0.6 pad_maximum_fusion.1.info_ref
  416.2 6.8 %shard_map.109 = bf16[128,3584]{1,0:T(8,128)(2,1)} custom-call(f32[4,128]{1,0:T(4,128)} %pad_maximum_fusion.1.info_ref, bf16[128,3584]{1,0:T(8,128)(2,1)} %bitcast.32, bf16[96,4,3584]{2,1,0:T(4,128)(2,1)} %copy-done.2), custom_call_target="tpu_custom_call" | custom-call | tf_op jit(solution)/shard_map/pallas_call | solution.py:251
  423.1 3.2 collective-permute-start.5
  426.3 0.0 copy-done.3
  426.3 0.0 copy-done.7
  426.3 0.1 collective-permute-start
  426.4 27.9 %collective-permute-done.info_ref = f32[4,128]{1,0:T(4,128)S(1)} collective-permute-done((f32[4,128]{1,0:T(4,128)S(1)}, f32[4,128]{1,0:T(4,128)S(1)}, u32[]{:S(2)}, u32[]{:S(2)}) %collective-permute-start) | collective-permute-done | bytes 2080 | tf_op jit(solution)/shard_map/ppermute | solution.py:30
  454.3 0.0 copy-start.5
  454.3 0.0 collective-permute-done.1.x_ref
  454.3 21.7 %all-to-all-done.1.back_ref = bf16[96,4,3584]{2,1,0:T(4,128)(2,1)S(1)} async-done(((bf16[96,4,3584]{2,1,0:T(4,128)(2,1)}), bf16[96,4,3584]{2,1,0:T(4,128)(2,1)S(1)}, u32[]{:S(2)}, u32[]{:S(2)}) %all-to-all-start.1) | async-done | bytes 2752544 | tf_op jit(solution)/shard_map/all_to_all | solution.py:211
  476.0 0.0 copy-done.5
  476.0 0.0 copy-start.1
  476.0 1.6 copy-done.1
  477.6 6.8 %shard_map.106 = bf16[128,3584]{1,0:T(8,128)(2,1)} custom-call(f32[4,128]{1,0:T(4,128)} %copy-done.5, bf16[128,3584]{1,0:T(8,128)(2,1)} %collective-permute-done.1.x_ref, bf16[96,4,3584]{2,1,0:T(4,128)(2,1)} %copy-done.1), custom_call_target="tpu_custom_call" | custom-call | tf_op jit(solution)/shard_map/pallas_call | solution.py:251
  484.4 0.0 collective-permute-done.5
  484.4 2.2 copy.12
  (3 shorter events, 0.0 us)
Async XLA Ops:
  8.3 134.2 %all-to-all-start.2 = ((bf16[192,4,3584]{2,1,0:T(4,128)(2,1)}), bf16[192,4,3584]{2,1,0:T(4,128)(2,1)}, u32[]{:S(2)}, u32[]{:S(2)}) async-start(bf16[192,4,3584]{2,1,0:T(4,128)(2,1)} %bitcast.23), calls=%async_computation.2 | async-start | bytes 11010048 | tf_op jit(solution)/shard_map/all_to_all | solution.py:211
  142.5 186.4 %all-to-all-start = ((bf16[96,4,3584]{2,1,0:T(4,128)(2,1)}), bf16[96,4,3584]{2,1,0:T(4,128)(2,1)}, u32[]{:S(2)}, u32[]{:S(2)}) async-start(bf16[96,4,3584]{2,1,0:T(4,128)(2,1)} %bitcast.30), calls=%async_computation | async-start | bytes 5505024 | tf_op jit(solution)/shard_map/all_to_all | solution.py:211
  154.7 82.5 %collective-permute-start.2 = (bf16[3584,512]{1,0:T(8,128)(2,1)}, bf16[3584,512]{1,0:T(8,128)(2,1)S(1)}, u32[]{:S(2)}, u32[]{:S(2)}) collective-permute-start(bf16[3584,512]{1,0:T(8,128)(2,1)} %bitcast.24), channel_id=1, source_target_pairs={{0,1},{1,0},{2,3},{3,2},{4,5},{5,4},{6,7},{7,6},{8,9},{9,8},{10,11... | collective-permute-start | bytes 11010056 | tf_op jit(solution)/shard_map/ppermute | solution.py:25
  154.8 158.6 %collective-permute-start.3 = (bf16[512,3584]{1,0:T(8,128)(2,1)}, bf16[512,3584]{1,0:T(8,128)(2,1)}, u32[]{:S(2)}, u32[]{:S(2)}) collective-permute-start(bf16[512,3584]{1,0:T(8,128)(2,1)} %bitcast.27), channel_id=1, source_target_pairs={{0,1},{1,0},{2,3},{3,2},{4,5},{5,4},{6,7},{7,6},{8,9},{9,8},{10,11... | collective-permute-start | bytes 11010056 | tf_op jit(solution)/shard_map/ppermute | solution.py:25
  237.2 76.2 %copy-start = (bf16[3584,512]{1,0:T(8,128)(2,1)}, bf16[3584,512]{1,0:T(8,128)(2,1)S(1)}, u32[]{:S(2)}) copy-start(bf16[3584,512]{1,0:T(8,128)(2,1)S(1)} %collective-permute-done.2.up_other) | copy-start | bytes 11010052
  328.9 75.8 %all-to-all-start.3 = ((bf16[96,4,3584]{2,1,0:T(4,128)(2,1)}), bf16[96,4,3584]{2,1,0:T(4,128)(2,1)S(1)}, u32[]{:S(2)}, u32[]{:S(2)}) async-start(bf16[96,4,3584]{2,1,0:T(4,128)(2,1)} %shard_map.108), calls=%async_computation.3 | async-start | bytes 5505024 | tf_op jit(solution)/shard_map/all_to_all | solution.py:211
  351.6 64.0 %copy-start.4 = (s32[1,128,2]{1,2,0:T(2,128)S(1)}, s32[1,128,2]{1,2,0:T(2,128)}, u32[]{:S(2)}) copy-start(s32[1,128,2]{1,2,0:T(2,128)} %param.14) | copy-start | bytes 3076
  351.7 64.0 %copy-start.6 = (f32[1,128,2]{1,2,0:T(2,128)S(1)}, f32[1,128,2]{1,2,0:T(2,128)}, u32[]{:S(2)}) copy-start(f32[1,128,2]{1,2,0:T(2,128)} %param.15) | copy-start | bytes 3076
  351.7 53.1 %collective-permute-start.4 = (bf16[96,4,3584]{2,1,0:T(4,128)(2,1)}, bf16[96,4,3584]{2,1,0:T(4,128)(2,1)}, u32[]{:S(2)}, u32[]{:S(2)}) collective-permute-start(bf16[96,4,3584]{2,1,0:T(4,128)(2,1)} %shard_map.105), channel_id=1, source_target_pairs={{0,64},{64,128},{128,192},{192,0},{1,65},{65,129},{129,193},{193,1... | collective-permute-start | bytes 8257544 | tf_op jit(solution)/shard_map/ppermute | solution.py:30
  404.7 1.6 copy-start.2
  406.3 69.7 %all-to-all-start.1 = ((bf16[96,4,3584]{2,1,0:T(4,128)(2,1)}), bf16[96,4,3584]{2,1,0:T(4,128)(2,1)S(1)}, u32[]{:S(2)}, u32[]{:S(2)}) async-start(bf16[96,4,3584]{2,1,0:T(4,128)(2,1)} %collective-permute-done.4), calls=%async_computation.1 | async-start | bytes 5505024 | tf_op jit(solution)/shard_map/all_to_all | solution.py:211
  415.5 10.8 %copy-start.3 = (s32[1,128,2]{1,2,0:T(2,128)S(1)}, s32[1,128,2]{1,2,0:T(2,128)}, u32[]{:S(2)}) copy-start(s32[1,128,2]{1,2,0:T(2,128)} %param.10) | copy-start | bytes 3076
  415.5 10.8 %copy-start.7 = (f32[1,128,2]{1,2,0:T(2,128)S(1)}, f32[1,128,2]{1,2,0:T(2,128)}, u32[]{:S(2)}) copy-start(f32[1,128,2]{1,2,0:T(2,128)} %param.11) | copy-start | bytes 3076
  415.5 38.8 %collective-permute-start.1 = (bf16[128,3584]{1,0:T(8,128)(2,1)}, bf16[128,3584]{1,0:T(8,128)(2,1)}, u32[]{:S(2)}, u32[]{:S(2)}) collective-permute-start(bf16[128,3584]{1,0:T(8,128)(2,1)} %bitcast.35), channel_id=1, source_target_pairs={{0,64},{64,128},{128,192},{192,0},{1,65},{65,129},{129,193},{193,1... | collective-permute-start | bytes 2752520 | tf_op jit(solution)/shard_map/ppermute | solution.py:30
  423.1 61.4 %collective-permute-start.5 = (bf16[1,128,3584]{2,1,0:T(8,128)(2,1)}, bf16[1,128,3584]{2,1,0:T(8,128)(2,1)}, u32[]{:S(2)}, u32[]{:S(2)}) collective-permute-start(bf16[1,128,3584]{2,1,0:T(8,128)(2,1)} %bitcast.36), channel_id=1, source_target_pairs={{0,192},{64,0},{128,64},{192,128},{1,193},{65,1},{129,65},{193,129... | collective-permute-start | bytes 2752520 | tf_op jit(solution)/shard_map/ppermute | solution.py:30
  426.3 28.0 %collective-permute-start = (f32[4,128]{1,0:T(4,128)S(1)}, f32[4,128]{1,0:T(4,128)S(1)}, u32[]{:S(2)}, u32[]{:S(2)}) collective-permute-start(f32[4,128]{1,0:T(4,128)S(1)} %pad_maximum_fusion), channel_id=1, source_target_pairs={{0,64},{64,128},{128,192},{192,0},{1,65},{65,129},{129,193},{193,1... | collective-permute-start | bytes 6152 | tf_op jit(solution)/shard_map/ppermute | solution.py:30
  454.3 21.7 %copy-start.5 = (f32[4,128]{1,0:T(4,128)}, f32[4,128]{1,0:T(4,128)S(1)}, u32[]{:S(2)}) copy-start(f32[4,128]{1,0:T(4,128)S(1)} %collective-permute-done.info_ref) | copy-start | bytes 6148
  476.0 1.6 copy-start.1

commit v5 on v4

--- a/solution.py
+++ b/solution.py
@@ -12,7 +12,7 @@
 ANY = pl.BlockSpec(memory_space=pl.ANY)
 AGAINST_ROWS = (((1,), (1,)), ((), ()))
 STEP = 512
-WIDE = 512
+WIDE = 1792
 
 
 def same_side_groups(devices):
@@ -51,19 +51,15 @@
     return jnp.where(named, before, -1.0)
 
 
-def slot_rows(place, block, first, capacity):
-    experts, _ = place.shape
-    rows = experts * block
+def slot_rows(place, capacity):
+    experts, tokens = place.shape
+    rows = experts * capacity
     row = lax.broadcasted_iota(jnp.int32, (rows, experts), 0)
-    col = lax.broadcasted_iota(jnp.int32, (rows, experts), 1)
-    begin = col * block + first
-    mine = (row >= begin) & (row < begin + capacity)
-    spread = mine.astype(jnp.float32).astype(jnp.bfloat16)
-    within = jnp.sum(jnp.where(mine, row - begin + 1, 0).astype(jnp.float32), 1, keepdims=True) - 1.0
-    slot = jnp.dot(
-        spread, (place + 1.0).astype(jnp.bfloat16), preferred_element_type=jnp.float32
-    ) - 1.0
-    return (slot == within) & (within >= 0.0)
+    begin = lax.broadcasted_iota(jnp.int32, (rows, experts), 1) * capacity
+    spread = as_bf16((row >= begin) & (row < begin + capacity))
+    slot = jnp.dot(spread, place.astype(jnp.bfloat16), preferred_element_type=jnp.float32)
+    row = lax.broadcasted_iota(jnp.int32, (rows, tokens), 0)
+    return slot == lax.rem(row, capacity).astype(jnp.float32)
 
 
 def as_bf16(mask):
@@ -82,7 +78,7 @@
     @pl.when(pl.program_id(0) == 0)
     def _():
         place = place_of(routes_ref[...], experts)
-        pick_ref[...] = as_bf16(slot_rows(place, capacity, 0, capacity))
+        pick_ref[...] = as_bf16(slot_rows(place, capacity))
 
     for i, x_ref in enumerate(x_refs):
         rows = jnp.dot(pick_ref[...], x_ref[...], preferred_element_type=jnp.float32)
@@ -153,29 +149,33 @@
         out_ref[:, :, c : c + STEP] = part.reshape(groups, per_group, STEP).astype(jnp.bfloat16)
 
 
-def combine_kernel(capacity, experts, info_ref, x_ref, back_ref, out_ref, pick_ref, weight_ref):
+def recipe_kernel(capacity, experts, info_ref, pick_ref, weight_ref):
+    routes = info_ref[0:2, :].astype(jnp.int32)
+    affinity = info_ref[2:4, :]
+    tokens = routes.shape[1]
+    rows = experts * capacity
+    pick = slot_rows(place_of(routes, experts), capacity)
+    row = lax.broadcasted_iota(jnp.int32, (rows, tokens), 0)
+    weights = affinity / jnp.sum(affinity, 0, keepdims=True)
+    for k in range(2):
+        begin = routes[k : k + 1, :] * capacity
+        mine = pick & (row >= begin) & (row < begin + capacity)
+        pick_ref[k * tokens : (k + 1) * tokens, :] = as_bf16(mine).T
+        weight_ref[k] = jnp.broadcast_to(weights[k : k + 1, :], (tokens, tokens)).T
+
+
+def combine_kernel(pick_ref, weight_ref, x_ref, back_ref, out_ref):
     tokens = x_ref.shape[0]
-    rows = experts * capacity
-
-    @pl.when(pl.program_id(0) == 0)
-    def _():
-        routes = info_ref[0:2, :].astype(jnp.int32)
-        affinity = info_ref[2:4, :]
-        pick = slot_rows(place_of(routes, experts), capacity, 0, capacity)
-        row = lax.broadcasted_iota(jnp.int32, (rows, tokens), 0)
-        weights = affinity / jnp.sum(affinity, 0, keepdims=True)
-        for k in range(2):
-            begin = routes[k : k + 1, :] * capacity
-            mine = pick & (row >= begin) & (row < begin + capacity)
-            pick_ref[k * tokens : (k + 1) * tokens, :] = as_bf16(mine).T
-            weight_ref[k] = jnp.broadcast_to(weights[k : k + 1, :], (tokens, tokens)).T
-
-    back = back_ref[...].reshape(rows, x_ref.shape[1])
+    back = back_ref[...].reshape(pick_ref.shape[1], x_ref.shape[1])
     picked = jnp.dot(pick_ref[...], back, preferred_element_type=jnp.float32)
     total = x_ref[...].astype(jnp.float32)
     for k in range(2):
         total = total + weight_ref[k, :, 0:1] * picked[k * tokens : (k + 1) * tokens]
     out_ref[...] = total.astype(jnp.bfloat16)
+
+
+def settle_kernel(in_ref, out_ref):
+    out_ref[...] = in_ref[...]
 
 
 def layer(
@@ -197,7 +197,7 @@
     capacity = 3 * tokens * top_count // devices
     rows = experts * capacity
     groups = same_side_groups(devices)
-    params = pltpu.CompilerParams(vmem_limit_bytes=60 * 1024 * 1024)
+    params = pltpu.CompilerParams(vmem_limit_bytes=63 * 1024 * 1024)
 
     up_own = up_weight[0]
     down_own = down_weight[0]
@@ -247,23 +247,40 @@
             compiler_params=params,
         )(received, up_own, down_own, up_other, down_other)
 
-    def combine(info, x, back):
+    def recipe(info):
         return pl.pallas_call(
-            functools.partial(combine_kernel, capacity, experts),
+            functools.partial(recipe_kernel, capacity, experts),
+            out_shape=(
+                jax.ShapeDtypeStruct((top_count * tokens, rows), jnp.bfloat16),
+                jax.ShapeDtypeStruct((top_count, tokens, tokens), jnp.float32),
+            ),
+            in_specs=[VMEM],
+            out_specs=(VMEM, VMEM),
+            compiler_params=params,
+        )(info)
+
+    def combine(pick_and_weight, x, back):
+        return pl.pallas_call(
+            combine_kernel,
             grid=(model_width // WIDE,),
             out_shape=jax.ShapeDtypeStruct((tokens, model_width), jnp.bfloat16),
             in_specs=[
-                pl.BlockSpec((2 * top_count, tokens), lambda i: (0, 0)),
+                pl.BlockSpec((top_count * tokens, rows), lambda i: (0, 0)),
+                pl.BlockSpec((top_count, tokens, tokens), lambda i: (0, 0, 0)),
                 pl.BlockSpec((tokens, WIDE), lambda i: (0, i)),
                 pl.BlockSpec((rows // 4, 4, WIDE), lambda i: (0, 0, i)),
             ],
             out_specs=pl.BlockSpec((tokens, WIDE), lambda i: (0, i)),
-            scratch_shapes=[
-                pltpu.VMEM((top_count * tokens, rows), jnp.bfloat16),
-                pltpu.VMEM((top_count, tokens, tokens), jnp.float32),
-            ],
             compiler_params=params,
-        )(info, x, back)
+        )(*pick_and_weight, x, back)
+
+    def settle(block):
+        return pl.pallas_call(
+            settle_kernel,
+            out_shape=jax.ShapeDtypeStruct(block.shape, block.dtype),
+            in_specs=[VMEM],
+            out_specs=VMEM,
+        )(block)
 
     def info_of(routes, affinity):
         return jnp.concatenate([routes.astype(jnp.float32), affinity[0].T], 0)
@@ -277,10 +294,13 @@
     served_f = shifted(served_f, "section", 1)
     back_f = exchange(served_f)
 
-    input_grad = combine(info_of(routes_b, affinity_bwd), grad_bwd[0], back_b)
-    bwd_next = shifted(input_grad[None], "section", -1)
-    fwd_next = combine(info_next, x_next, back_f)
-    return (fwd_next[None], bwd_next)
+    recipe_b = recipe(info_of(routes_b, affinity_bwd))
+    recipe_f = recipe(info_next)
+    input_grad = combine(recipe_b, grad_bwd[0], back_b)
+    bwd_next = shifted(input_grad, "section", -1)
+    bwd_next = settle(bwd_next)
+    fwd_next = combine(recipe_f, x_next, back_f)
+    return (fwd_next[None], bwd_next[None])
 
 
 def solution(mesh):

time: 490 us -> 481 us (0.982)
  Pallas kernels: 55.5 us -> 49.6 us
    pallas_call x2, Pallas kernels: 13.9 us -> 8.76 us  [dispatch(): pl.pallas_call(functools.partial(dispatch_kernel, capacity, experts, coun...]
    pallas_call x2 -> x5, Pallas kernels: 13.7 us -> 13.1 us  [the longest x2 7.37 us: combine(): pl.pallas_call(combine_kernel, grid=(model_width // WIDE,), out_shape=jax...]
  transfers between devices with their start and end apart: 10 -> 10, of which waited for: 6 -> 6; matrix products, arithmetic and copies ran while one was open for 0% -> 0% of each run, Pallas kernels for 10% -> 9%
where the time goes in v5:
time: 481 us; the launch traced here: 478 us
  waiting for transfers between devices  377 us (78%)
  starting transfers between devices  49.7 us (10%)
  Pallas kernels  49.6 us (10%)
    ppermute x2, waiting for transfers between devices, from_partner(): return lax.ppermute(block, axis, [(i, i ^ 1) for i in range(count)])  157 us
    all_to_all x4, waiting for transfers between devices, exchange(): lax.all_to_all(block, 'expert', split_axis=0, concat_axis=0, tiled=True,...  137 us
    ppermute x4, waiting for transfers between devices, shifted(): lax.ppermute(shard, axis, [(i, (i + by) % size) for i in range(size)])  82.8 us
    all_to_all x4, starting transfers between devices, exchange(): lax.all_to_all(block, 'expert', split_axis=0, concat_axis=0, tiled=True,...  44.1 us
    pallas_call x2, Pallas kernels, serve(): pl.pallas_call(kernel, out_shape=jax.ShapeDtypeStruct((rows // 4, 4, mode...  27.8 us
  transfers between devices with their start and end apart: 10, of which 6 were waited for; matrix products, arithmetic and copies ran while one was open for 0% of the time, Pallas kernels for 9%

profile of v5, /device:TPU:24, one launch (start us, length us, event | category | flops | bytes accessed | tf_op | source)
XLA Modules:
  0.0 477.8 jit_solution(18287498655634919133)
XLA Ops:
  0.6 5.1 %shard_map.109 = bf16[32,6,4,3584]{3,2,1,0:T(4,128)(2,1)} custom-call(s32[2,128]{1,0:T(2,128)} %bitcast.37, bf16[128,3584]{1,0:T(8,128)(2,1)} %bitcast.35, bf16[128,3584]{1,0:T(8,128)(2,1)} %bitcast.31), custom_call_target="tpu_custom_call" | custom-call | tf_op jit(solution)/shard_map/pallas_call | solution.py:218
  5.7 12.3 %all-to-all-start.2 = ((bf16[192,4,3584]{2,1,0:T(4,128)(2,1)}), bf16[192,4,3584]{2,1,0:T(4,128)(2,1)}, u32[]{:S(2)}, u32[]{:S(2)}) async-start(bf16[192,4,3584]{2,1,0:T(4,128)(2,1)} %bitcast.23), calls=%async_computation.2 | async-start | bytes 11010048 | tf_op jit(solution)/shard_map/all_to_all | solution.py:211
  18.0 3.7 shard_map.105
  21.7 118.2 %all-to-all-done.2.recv_ref = bf16[192,4,3584]{2,1,0:T(4,128)(2,1)} async-done(((bf16[192,4,3584]{2,1,0:T(4,128)(2,1)}), bf16[192,4,3584]{2,1,0:T(4,128)(2,1)}, u32[]{:S(2)}, u32[]{:S(2)}) %all-to-all-start.2) | async-done | bytes 5505056 | tf_op jit(solution)/shard_map/all_to_all | solution.py:211
  139.9 12.2 %all-to-all-start = ((bf16[96,4,3584]{2,1,0:T(4,128)(2,1)}), bf16[96,4,3584]{2,1,0:T(4,128)(2,1)}, u32[]{:S(2)}, u32[]{:S(2)}) async-start(bf16[96,4,3584]{2,1,0:T(4,128)(2,1)} %bitcast.30), calls=%async_computation | async-start | bytes 5505024 | tf_op jit(solution)/shard_map/all_to_all | solution.py:211
  152.0 0.1 collective-permute-start.2
  152.1 2.0 collective-permute-start.3
  154.2 80.5 %collective-permute-done.2.up_other = bf16[3584,512]{1,0:T(8,128)(2,1)} collective-permute-done((bf16[3584,512]{1,0:T(8,128)(2,1)}, bf16[3584,512]{1,0:T(8,128)(2,1)}, u32[]{:S(2)}, u32[]{:S(2)}) %collective-permute-start.2) | collective-permute-done | bytes 3670048 | tf_op jit(solution)/shard_map/ppermute | solution.py:25
  234.7 76.0 %collective-permute-done.3.down_other = bf16[512,3584]{1,0:T(8,128)(2,1)} collective-permute-done((bf16[512,3584]{1,0:T(8,128)(2,1)}, bf16[512,3584]{1,0:T(8,128)(2,1)}, u32[]{:S(2)}, u32[]{:S(2)}) %collective-permute-start.3) | collective-permute-done | bytes 3670048 | tf_op jit(solution)/shard_map/ppermute | solution.py:25
  310.7 15.6 %shard_map.110 = bf16[96,4,3584]{2,1,0:T(4,128)(2,1)} custom-call(bf16[192,4,3584]{2,1,0:T(4,128)(2,1)} %all-to-all-done.2.recv_ref, bf16[3584,512]{1,0:T(8,128)(2,1)} %bitcast.25, bf16[512,3584]{1,0:T(8,128)(2,1)} %bitcast.28, bf16[3584,512]{1,0:T(8,128)(2,1)} %collective-permute-done.2.up_other, bf16[512,3584]{1,0:T(8,128)(2,1)} %collective-permute-done.3.down_other), custom_call_target="tpu_custom_call" | custom-call | tf_op jit(solution)/shard_map/pallas_call | solution.py:236
  326.3 0.0 all-to-all-done.recv_ref
  326.3 10.5 %all-to-all-start.3 = ((bf16[96,4,3584]{2,1,0:T(4,128)(2,1)}), bf16[96,4,3584]{2,1,0:T(4,128)(2,1)}, u32[]{:S(2)}, u32[]{:S(2)}) async-start(bf16[96,4,3584]{2,1,0:T(4,128)(2,1)} %shard_map.110), calls=%async_computation.3 | async-start | bytes 5505024 | tf_op jit(solution)/shard_map/all_to_all | solution.py:211
  336.8 12.2 %shard_map.106 = bf16[96,4,3584]{2,1,0:T(4,128)(2,1)} custom-call(bf16[96,4,3584]{2,1,0:T(4,128)(2,1)} %all-to-all-done.recv_ref, bf16[3584,512]{1,0:T(8,128)(2,1)} %bitcast.26, bf16[512,3584]{1,0:T(8,128)(2,1)} %bitcast.29, bf16[3584,512]{1,0:T(8,128)(2,1)} %collective-permute-done.2.up_other, bf16[512,3584]{1,0:T(8,128)(2,1)} %collective-permute-done.3.down_other), custom_call_target="tpu_custom_call" | custom-call | tf_op jit(solution)/shard_map/pallas_call | solution.py:236
  349.0 0.0 copy-start.2
  349.0 0.0 copy-start.4
  349.0 0.1 collective-permute-start.4
  349.1 53.0 %collective-permute-done.4 = bf16[96,4,3584]{2,1,0:T(4,128)(2,1)} collective-permute-done((bf16[96,4,3584]{2,1,0:T(4,128)(2,1)}, bf16[96,4,3584]{2,1,0:T(4,128)(2,1)}, u32[]{:S(2)}, u32[]{:S(2)}) %collective-permute-start.4) | collective-permute-done | bytes 2752544 | tf_op jit(solution)/shard_map/ppermute | solution.py:30
  402.1 0.0 all-to-all-done.3.back_ref
  402.1 9.2 %all-to-all-start.1 = ((bf16[96,4,3584]{2,1,0:T(4,128)(2,1)}), bf16[96,4,3584]{2,1,0:T(4,128)(2,1)}, u32[]{:S(2)}, u32[]{:S(2)}) async-start(bf16[96,4,3584]{2,1,0:T(4,128)(2,1)} %collective-permute-done.4), calls=%async_computation.1 | async-start | bytes 5505024 | tf_op jit(solution)/shard_map/all_to_all | solution.py:211
  411.3 0.0 copy-start.1
  411.3 0.0 copy-start.5
  411.3 0.1 collective-permute-start.1
  411.4 0.0 copy-done.2
  411.4 0.0 copy-done.4
  411.5 0.6 pad_maximum_fusion.1.info_ref
  412.0 1.8 shard_map.108
  413.8 3.7 shard_map.111
  417.5 3.2 collective-permute-start.5
  420.7 0.0 copy-done.1
  420.7 0.0 copy-done.5
  420.8 0.1 collective-permute-start
  420.9 29.8 %collective-permute-done.info_ref = f32[4,128]{1,0:T(4,128)S(1)} collective-permute-done((f32[4,128]{1,0:T(4,128)S(1)}, f32[4,128]{1,0:T(4,128)S(1)}, u32[]{:S(2)}, u32[]{:S(2)}) %collective-permute-start) | collective-permute-done | bytes 2080 | tf_op jit(solution)/shard_map/ppermute | solution.py:30
  450.6 0.0 copy-start.3
  450.6 0.6 copy-done.3
  451.2 1.8 shard_map.104
  453.0 0.0 collective-permute-done.1.x_ref
  453.0 0.0 copy-start
  453.0 19.0 %all-to-all-done.1.back_ref = bf16[96,4,3584]{2,1,0:T(4,128)(2,1)} async-done(((bf16[96,4,3584]{2,1,0:T(4,128)(2,1)}), bf16[96,4,3584]{2,1,0:T(4,128)(2,1)}, u32[]{:S(2)}, u32[]{:S(2)}) %all-to-all-start.1) | async-done | bytes 2752544 | tf_op jit(solution)/shard_map/all_to_all | solution.py:211
  472.0 0.0 copy-done
  472.0 3.7 shard_map.107
  475.7 0.0 collective-permute-done.5.in_ref
  475.7 2.2 shard_map.112
  (3 shorter events, 0.0 us)
Async XLA Ops:
  5.7 134.2 %all-to-all-start.2 = ((bf16[192,4,3584]{2,1,0:T(4,128)(2,1)}), bf16[192,4,3584]{2,1,0:T(4,128)(2,1)}, u32[]{:S(2)}, u32[]{:S(2)}) async-start(bf16[192,4,3584]{2,1,0:T(4,128)(2,1)} %bitcast.23), calls=%async_computation.2 | async-start | bytes 11010048 | tf_op jit(solution)/shard_map/all_to_all | solution.py:211
  139.9 186.4 %all-to-all-start = ((bf16[96,4,3584]{2,1,0:T(4,128)(2,1)}), bf16[96,4,3584]{2,1,0:T(4,128)(2,1)}, u32[]{:S(2)}, u32[]{:S(2)}) async-start(bf16[96,4,3584]{2,1,0:T(4,128)(2,1)} %bitcast.30), calls=%async_computation | async-start | bytes 5505024 | tf_op jit(solution)/shard_map/all_to_all | solution.py:211
  152.0 82.6 %collective-permute-start.2 = (bf16[3584,512]{1,0:T(8,128)(2,1)}, bf16[3584,512]{1,0:T(8,128)(2,1)}, u32[]{:S(2)}, u32[]{:S(2)}) collective-permute-start(bf16[3584,512]{1,0:T(8,128)(2,1)} %bitcast.24), channel_id=1, source_target_pairs={{0,1},{1,0},{2,3},{3,2},{4,5},{5,4},{6,7},{7,6},{8,9},{9,8},{10,11... | collective-permute-start | bytes 11010056 | tf_op jit(solution)/shard_map/ppermute | solution.py:25
  152.1 158.6 %collective-permute-start.3 = (bf16[512,3584]{1,0:T(8,128)(2,1)}, bf16[512,3584]{1,0:T(8,128)(2,1)}, u32[]{:S(2)}, u32[]{:S(2)}) collective-permute-start(bf16[512,3584]{1,0:T(8,128)(2,1)} %bitcast.27), channel_id=1, source_target_pairs={{0,1},{1,0},{2,3},{3,2},{4,5},{5,4},{6,7},{7,6},{8,9},{9,8},{10,11... | collective-permute-start | bytes 11010056 | tf_op jit(solution)/shard_map/ppermute | solution.py:25
  326.3 75.8 %all-to-all-start.3 = ((bf16[96,4,3584]{2,1,0:T(4,128)(2,1)}), bf16[96,4,3584]{2,1,0:T(4,128)(2,1)}, u32[]{:S(2)}, u32[]{:S(2)}) async-start(bf16[96,4,3584]{2,1,0:T(4,128)(2,1)} %shard_map.110), calls=%async_computation.3 | async-start | bytes 5505024 | tf_op jit(solution)/shard_map/all_to_all | solution.py:211
  349.0 62.4 %copy-start.2 = (s32[1,128,2]{1,2,0:T(2,128)S(1)}, s32[1,128,2]{1,2,0:T(2,128)}, u32[]{:S(2)}) copy-start(s32[1,128,2]{1,2,0:T(2,128)} %param.14) | copy-start | bytes 3076
  349.0 62.5 %copy-start.4 = (f32[1,128,2]{1,2,0:T(2,128)S(1)}, f32[1,128,2]{1,2,0:T(2,128)}, u32[]{:S(2)}) copy-start(f32[1,128,2]{1,2,0:T(2,128)} %param.15) | copy-start | bytes 3076
  349.0 53.1 %collective-permute-start.4 = (bf16[96,4,3584]{2,1,0:T(4,128)(2,1)}, bf16[96,4,3584]{2,1,0:T(4,128)(2,1)}, u32[]{:S(2)}, u32[]{:S(2)}) collective-permute-start(bf16[96,4,3584]{2,1,0:T(4,128)(2,1)} %shard_map.106), channel_id=1, source_target_pairs={{0,64},{64,128},{128,192},{192,0},{1,65},{65,129},{129,193},{193,1... | collective-permute-start | bytes 8257544 | tf_op jit(solution)/shard_map/ppermute | solution.py:30
  402.1 69.9 %all-to-all-start.1 = ((bf16[96,4,3584]{2,1,0:T(4,128)(2,1)}), bf16[96,4,3584]{2,1,0:T(4,128)(2,1)}, u32[]{:S(2)}, u32[]{:S(2)}) async-start(bf16[96,4,3584]{2,1,0:T(4,128)(2,1)} %collective-permute-done.4), calls=%async_computation.1 | async-start | bytes 5505024 | tf_op jit(solution)/shard_map/all_to_all | solution.py:211
  411.3 9.4 %copy-start.1 = (s32[1,128,2]{1,2,0:T(2,128)S(1)}, s32[1,128,2]{1,2,0:T(2,128)}, u32[]{:S(2)}) copy-start(s32[1,128,2]{1,2,0:T(2,128)} %param.10) | copy-start | bytes 3076
  411.3 9.4 %copy-start.5 = (f32[1,128,2]{1,2,0:T(2,128)S(1)}, f32[1,128,2]{1,2,0:T(2,128)}, u32[]{:S(2)}) copy-start(f32[1,128,2]{1,2,0:T(2,128)} %param.11) | copy-start | bytes 3076
  411.3 41.7 %collective-permute-start.1 = (bf16[128,3584]{1,0:T(8,128)(2,1)}, bf16[128,3584]{1,0:T(8,128)(2,1)S(1)}, u32[]{:S(2)}, u32[]{:S(2)}) collective-permute-start(bf16[128,3584]{1,0:T(8,128)(2,1)} %bitcast.4.refs_1_), channel_id=1, source_target_pairs={{0,64},{64,128},{128,192},{192,0},{1,65},{65,129},{129,193},{193,1... | collective-permute-start | bytes 2752520 | tf_op jit(solution)/shard_map/ppermute | solution.py:30
  417.5 58.2 %collective-permute-start.5 = (bf16[128,3584]{1,0:T(8,128)(2,1)}, bf16[128,3584]{1,0:T(8,128)(2,1)}, u32[]{:S(2)}, u32[]{:S(2)}) collective-permute-start(bf16[128,3584]{1,0:T(8,128)(2,1)} %shard_map.111), channel_id=1, source_target_pairs={{0,192},{64,0},{128,64},{192,128},{1,193},{65,1},{129,65},{193,129... | collective-permute-start | bytes 2752520 | tf_op jit(solution)/shard_map/ppermute | solution.py:30
  420.8 29.9 %collective-permute-start = (f32[4,128]{1,0:T(4,128)S(1)}, f32[4,128]{1,0:T(4,128)S(1)}, u32[]{:S(2)}, u32[]{:S(2)}) collective-permute-start(f32[4,128]{1,0:T(4,128)S(1)} %pad_maximum_fusion), channel_id=1, source_target_pairs={{0,64},{64,128},{128,192},{192,0},{1,65},{65,129},{129,193},{193,1... | collective-permute-start | bytes 6152 | tf_op jit(solution)/shard_map/ppermute | solution.py:30
  450.6 0.6 copy-start.3
  453.0 19.0 %copy-start = (bf16[128,3584]{1,0:T(8,128)(2,1)}, bf16[128,3584]{1,0:T(8,128)(2,1)S(1)}, u32[]{:S(2)}) copy-start(bf16[128,3584]{1,0:T(8,128)(2,1)S(1)} %collective-permute-done.1.x_ref) | copy-start | bytes 2752516

commit v6 on v5

--- a/solution.py
+++ b/solution.py
@@ -12,6 +12,7 @@
 ANY = pl.BlockSpec(memory_space=pl.ANY)
 AGAINST_ROWS = (((1,), (1,)), ((), ()))
 STEP = 512
+BATCHES = ((4, 3, 5, 0), (2, 6, 1, 7))
 WIDE = 1792
 
 
@@ -83,6 +84,49 @@
     for i, x_ref in enumerate(x_refs):
         rows = jnp.dot(pick_ref[...], x_ref[...], preferred_element_type=jnp.float32)
         write_groups(out_ref, i * capacity // 4, rows, experts)
+
+
+def relative_routes(routes):
+    me = lax.axis_index("expert")
+    x, z, member = me // 32, (me // 4) % 8, (me % 4) // 2
+    plane = ((routes // 2) % 8 - z + 8) % 8
+    return plane * 4 + ((routes // 16) ^ x) * 2 + ((routes % 2) ^ member)
+
+
+def dispatch_planes_kernel(capacity, experts, routes_ref, x_ref, g_ref, *refs):
+    out_refs, pick_ref = refs[:-1], refs[-1]
+
+    @pl.when(pl.program_id(0) == 0)
+    def _():
+        place = place_of(relative_routes(routes_ref[...]), experts)
+        pick_ref[...] = as_bf16(slot_rows(place, capacity))
+
+    planes = len(out_refs)
+    members, groups = experts // planes, capacity // 4
+    for i, rows_ref in enumerate((x_ref, g_ref)):
+        rows = jnp.dot(pick_ref[...], rows_ref[...], preferred_element_type=jnp.float32)
+        blocks = rows.reshape(planes, members, groups, 4, rows.shape[1]).astype(jnp.bfloat16)
+        for k, out_ref in enumerate(out_refs):
+            out_ref[:, i * groups : (i + 1) * groups] = blocks[k]
+
+
+def regroup_kernel(block, *refs):
+    count = (len(refs) - 1) // 2
+    in_refs, out_refs, sems = refs[:count], refs[count : 2 * count], refs[-1]
+    copies = []
+    for i, out_ref in enumerate(out_refs):
+        for k, in_ref in enumerate(in_refs):
+            copies.append(
+                pltpu.make_async_copy(
+                    in_ref.at[pl.ds(i * block, block)],
+                    out_ref.at[pl.ds(k * block, block)],
+                    sems.at[i, k],
+                )
+            )
+    for copy in copies:
+        copy.start()
+    for copy in copies:
+        copy.wait()
 
 
 def start_loads(up_own, down_own, up_other, down_other, ups, downs, sems):
@@ -117,26 +161,38 @@
         out_ref[:, :, c : c + STEP] = part.reshape(groups, per_group, STEP).astype(jnp.bfloat16)
 
 
-def expert_bwd_kernel(
-    recv_ref, up_own, down_own, up_other, down_other, out_ref, ups, downs, hidden, sems
-):
+def expert_bwd_kernel(batches, *refs):
+    count = len(batches) * 4
+    recv_refs = refs[:count]
+    up_own, down_own, up_other, down_other, out_ref = refs[count : count + 5]
+    ups, downs, hidden, sems, x_ref, g_ref = refs[count + 5 :]
     groups, per_group, width = out_ref.shape
-    rows = groups * per_group
     half = hidden.shape[1] // 2
     loads = start_loads(up_own, down_own, up_other, down_other, ups, downs, sems)
-    sources = hidden.shape[1] // 32
-    both = recv_ref[...].reshape(sources, 2 * groups // sources, per_group, width)
-    x = both[:, : groups // sources].reshape(rows, width)
-    g = both[:, groups // sources :].reshape(rows, width)
+    planes = len(batches[0])
+    each = x_ref.shape[0] // count
+    for n, recv_ref in enumerate(recv_refs):
+        both = recv_ref[...].reshape(planes, 2, each // planes // 4, per_group, width)
+        x_ref[n * each : (n + 1) * each, :] = both[:, 0].reshape(each, width)
+        g_ref[n * each : (n + 1) * each, :] = both[:, 1].reshape(each, width)
     for i in range(2):
         loads[2 * i].wait()
-        pre_act = jnp.dot(x, ups[i], preferred_element_type=jnp.float32)
+        pre_act = jnp.dot(x_ref[...], ups[i], preferred_element_type=jnp.float32)
         loads[2 * i + 1].wait()
         hidden_grad = lax.dot_general(
-            g, downs[i], AGAINST_ROWS, preferred_element_type=jnp.float32
+            g_ref[...], downs[i], AGAINST_ROWS, preferred_element_type=jnp.float32
         )
         pre_grad = hidden_grad * silu_grad(pre_act)
         hidden[:, i * half : (i + 1) * half] = pre_grad.astype(jnp.bfloat16)
+    me = lax.axis_index("expert")
+    x, z, member = me // 32, (me // 4) % 8, (me % 4) // 2
+    sources = [
+        (x ^ (i // 2)) * 16 + ((z - k + 8) % 8) * 2 + (member ^ (i % 2))
+        for batch in batches
+        for i in range(4)
+        for k in batch
+    ]
+    piece = groups // len(sources)
     for c in range(0, width, STEP):
         part = lax.dot_general(
             hidden[:, :half], ups[0, c : c + STEP, :], AGAINST_ROWS,
@@ -146,7 +202,9 @@
             hidden[:, half:], ups[1, c : c + STEP, :], AGAINST_ROWS,
             preferred_element_type=jnp.float32,
         )
-        out_ref[:, :, c : c + STEP] = part.reshape(groups, per_group, STEP).astype(jnp.bfloat16)
+        blocks = part.reshape(len(sources), piece, per_group, STEP).astype(jnp.bfloat16)
+        for n, source in enumerate(sources):
+            out_ref[pl.ds(source * piece, piece), :, c : c + STEP] = blocks[n]
 
 
 def recipe_kernel(capacity, experts, info_ref, pick_ref, weight_ref):
@@ -227,25 +285,67 @@
         )(routes, *blocks)
         return sent.reshape(experts * groups_out, 4, model_width)
 
-    recv_b = exchange(dispatch(routes_b, (x_bwd[0], grad_bwd[0])))
+    groups_b = 2 * capacity // 4
+    sent_b = pl.pallas_call(
+        functools.partial(dispatch_planes_kernel, capacity, experts),
+        grid=(model_width // WIDE,),
+        out_shape=[jax.ShapeDtypeStruct((4, groups_b, 4, model_width), jnp.bfloat16)] * 8,
+        in_specs=[pl.BlockSpec((top_count, tokens), lambda i: (0, 0))]
+        + [pl.BlockSpec((tokens, WIDE), lambda i: (0, i))] * 2,
+        out_specs=[pl.BlockSpec((4, groups_b, 4, WIDE), lambda i: (0, 0, 0, i))] * 8,
+        scratch_shapes=[pltpu.VMEM((rows, tokens), jnp.bfloat16)],
+        compiler_params=params,
+        name="dispatch_bwd",
+    )(routes_b, x_bwd[0], grad_bwd[0])
+    sent_b = [block.reshape(4 * groups_b, 4, model_width) for block in sent_b]
+
+    def along_z(block, k):
+        pairs = [(d, d // 32 * 32 + (d + 4 * k) % 32) for d in range(devices)]
+        return lax.ppermute(block, "expert", pairs)
+
+    def in_plane(block, i):
+        pairs = [
+            (d, (d ^ (32 * (i // 2))) // 4 * 4 + (3 - d % 4 if i % 2 else d % 4))
+            for d in range(devices)
+        ]
+        return lax.ppermute(block, "expert", pairs)
+
+    def regroup(blocks):
+        count = len(blocks)
+        return pl.pallas_call(
+            functools.partial(regroup_kernel, groups_b),
+            out_shape=[jax.ShapeDtypeStruct(blocks[0].shape, jnp.bfloat16)] * count,
+            in_specs=[ANY] * count,
+            out_specs=[ANY] * count,
+            scratch_shapes=[pltpu.SemaphoreType.DMA((count, count))],
+            compiler_params=params,
+        )(*blocks)
+
+    arrived = {k: along_z(sent_b[k], k) for batch in BATCHES for k in batch if k}
+    arrived[0] = sent_b[0]
+    recv_b = []
+    for batch in BATCHES:
+        by_member = regroup([arrived[k] for k in batch])
+        recv_b += [in_plane(block, i) if i else block for i, block in enumerate(by_member)]
     recv_f = exchange(dispatch(routes_f, (x_fwd[0],)))
 
     half = up_own.shape[1]
 
-    def serve(kernel, received):
+    def serve(kernel, received, extra=()):
         return pl.pallas_call(
             kernel,
             out_shape=jax.ShapeDtypeStruct((rows // 4, 4, model_width), jnp.bfloat16),
-            in_specs=[VMEM] + [ANY] * 4,
+            in_specs=[VMEM] * len(received) + [ANY] * 4,
             out_specs=VMEM,
             scratch_shapes=[
                 pltpu.VMEM((2, model_width, half), jnp.bfloat16),
                 pltpu.VMEM((2, half, model_width), jnp.bfloat16),
                 pltpu.VMEM((rows, 2 * half), jnp.bfloat16),
                 pltpu.SemaphoreType.DMA((4,)),
+                *extra,
             ],
             compiler_params=params,
-        )(received, up_own, down_own, up_other, down_other)
+        )(*received, up_own, down_own, up_other, down_other)
 
     def recipe(info):
         return pl.pallas_call(
@@ -285,12 +385,16 @@
     def info_of(routes, affinity):
         return jnp.concatenate([routes.astype(jnp.float32), affinity[0].T], 0)
 
-    served_b = serve(expert_bwd_kernel, recv_b)
+    served_b = serve(
+        functools.partial(expert_bwd_kernel, BATCHES),
+        recv_b,
+        [pltpu.VMEM((rows, model_width), jnp.bfloat16)] * 2,
+    )
     back_b = exchange(served_b)
 
     x_next = shifted(x_fwd[0], "section", 1)
     info_next = shifted(info_of(routes_f, affinity_fwd), "section", 1)
-    served_f = serve(expert_fwd_kernel, recv_f)
+    served_f = serve(expert_fwd_kernel, [recv_f])
     served_f = shifted(served_f, "section", 1)
     back_f = exchange(served_f)
 

time: 481 us -> 519 us (1.079)
  Pallas kernels: 49.6 us -> 219 us
  waiting for transfers between devices: 377 us -> 234 us
  starting transfers between devices: 49.7 us -> 58.5 us
    pallas_call x0 -> x3, Pallas kernels: none -> 174 us  [the longest x2 169 us: regroup(): pl.pallas_call(functools.partial(regroup_kernel, groups_b), out_shape=[ja...]
    ppermute x2, waiting for transfers between devices: 157 us -> 0.01 us  [from_partner(): return lax.ppermute(block, axis, [(i, i ^ 1) for i in range(count)])]
    ppermute x0 -> x13, waiting for transfers between devices: none -> 145 us  [the longest x7 122 us: along_z(): return lax.ppermute(block, 'expert', pairs)]
    all_to_all x4 -> x3, waiting for transfers between devices: 137 us -> 10.9 us  [exchange(): lax.all_to_all(block, 'expert', split_axis=0, concat_axis=0, tiled=True,...]
    ppermute x0 -> x13, starting transfers between devices: none -> 24.2 us  [the longest x7 14.7 us: along_z(): return lax.ppermute(block, 'expert', pairs)]
    all_to_all x4 -> x3, starting transfers between devices: 44.1 us -> 29.9 us  [exchange(): lax.all_to_all(block, 'expert', split_axis=0, concat_axis=0, tiled=True,...]
  transfers between devices with their start and end apart: 10 -> 22, of which waited for: 6 -> 8; matrix products, arithmetic and copies ran while one was open for 0% -> 0% of each run, Pallas kernels for 9% -> 41%
where the time goes in v6:
time: 519 us; the launch traced here: 515 us
  waiting for transfers between devices  234 us (45%)
  Pallas kernels  219 us (42%)
  starting transfers between devices  58.5 us (11%)
    pallas_call x2, Pallas kernels, regroup(): pl.pallas_call(functools.partial(regroup_kernel, groups_b), out_shape=[ja...  169 us
    ppermute x7, waiting for transfers between devices, along_z(): return lax.ppermute(block, 'expert', pairs)  122 us
    ppermute x4, waiting for transfers between devices, shifted(): lax.ppermute(shard, axis, [(i, (i + by) % size) for i in range(size)])  78.6 us
    all_to_all x3, starting transfers between devices, exchange(): lax.all_to_all(block, 'expert', split_axis=0, concat_axis=0, tiled=True,...  29.9 us
    pallas_call x2, Pallas kernels, serve(): pl.pallas_call(kernel, out_shape=jax.ShapeDtypeStruct((rows // 4, 4, mode...  27.8 us
    ppermute x6, waiting for transfers between devices, in_plane(): return lax.ppermute(block, 'expert', pairs)  22.5 us
    ppermute x7, starting transfers between devices, along_z(): return lax.ppermute(block, 'expert', pairs)  14.7 us
    all_to_all x3, waiting for transfers between devices, exchange(): lax.all_to_all(block, 'expert', split_axis=0, concat_axis=0, tiled=True,...  10.9 us
  transfers between devices with their start and end apart: 22, of which 8 were waited for; matrix products, arithmetic and copies ran while one was open for 0% of the time, Pallas kernels for 41%

profile of v6, /device:TPU:24, one launch (start us, length us, event | category | flops | bytes accessed | tf_op | source)
XLA Modules:
  0.0 515.3 jit_solution(18358046302480782824)
XLA Ops:
  0.6 3.7 shard_map.105
  4.3 12.3 %all-to-all-start = ((bf16[96,4,3584]{2,1,0:T(4,128)(2,1)}), bf16[96,4,3584]{2,1,0:T(4,128)(2,1)}, u32[]{:S(2)}, u32[]{:S(2)}) async-start(bf16[96,4,3584]{2,1,0:T(4,128)(2,1)} %bitcast.36), calls=%async_computation | async-start | bytes 5505024 | tf_op jit(solution)/shard_map/all_to_all | solution.py:269
  16.6 0.1 collective-permute-start.2
  16.7 2.0 collective-permute-start.3
  18.7 4.9 dispatch_bwd.1
  23.6 2.4 collective-permute-start.11
  26.0 1.8 collective-permute-start.12
  27.8 1.5 collective-permute-start.13
  29.2 80.2 %collective-permute-done.11.refs_0_ = bf16[24,4,3584]{2,1,0:T(4,128)(2,1)S(1)} collective-permute-done((bf16[24,4,3584]{2,1,0:T(4,128)(2,1)}, bf16[24,4,3584]{2,1,0:T(4,128)(2,1)S(1)}, u32[]{:S(2)}, u32[]{:S(2)}) %collective-permute-start.11) | collective-permute-done | bytes 688160 | tf_op jit(solution)/shard_map/ppermute | solution.py:304
  109.4 1.3 collective-permute-start.14
  110.8 0.9 copy-done.4
  111.7 1.1 collective-permute-start.5
  112.7 10.1 %collective-permute-done.13.refs_2_ = bf16[24,4,3584]{2,1,0:T(4,128)(2,1)} collective-permute-done((bf16[24,4,3584]{2,1,0:T(4,128)(2,1)}, bf16[24,4,3584]{2,1,0:T(4,128)(2,1)}, u32[]{:S(2)}, u32[]{:S(2)}) %collective-permute-start.13) | collective-permute-done | bytes 688160 | tf_op jit(solution)/shard_map/ppermute | solution.py:304
  122.8 2.7 collective-permute-start.6
  125.5 32.1 %collective-permute-done.14.refs_3_ = bf16[24,4,3584]{2,1,0:T(4,128)(2,1)} collective-permute-done((bf16[24,4,3584]{2,1,0:T(4,128)(2,1)}, bf16[24,4,3584]{2,1,0:T(4,128)(2,1)}, u32[]{:S(2)}, u32[]{:S(2)}) %collective-permute-start.14) | collective-permute-done | bytes 688160 | tf_op jit(solution)/shard_map/ppermute | solution.py:304
  157.5 4.0 collective-permute-start.7
  161.5 84.6 %shard_map.110 = (bf16[24,4,3584]{2,1,0:T(4,128)(2,1)}, bf16[24,4,3584]{2,1,0:T(4,128)(2,1)}, bf16[24,4,3584]{2,1,0:T(4,128)(2,1)}, bf16[24,4,3584]{2,1,0:T(4,128)(2,1)}) custom-call(bf16[24,4,3584]{2,1,0:T(4,128)(2,1)} %copy-done.3, bf16[24,4,3584]{2,1,0:T(4,128)(2,1)} %copy-done.4, bf16[24,4,3584]{2,1,0:T(4,128)(2,1)} %collective-permute-done.13.refs_2_, ...), custom_call_target="tpu_custom_call" | custom-call | tf_op jit(solution)/shard_map/pallas_call | solution.py:315
  246.1 0.0 copy-start.2
  246.2 0.8 copy-done.2
  247.0 0.2 collective-permute-start.15
  247.2 1.8 collective-permute-start.16
  249.1 2.6 collective-permute-start.17
  251.7 84.6 %shard_map.109 = (bf16[24,4,3584]{2,1,0:T(4,128)(2,1)}, bf16[24,4,3584]{2,1,0:T(4,128)(2,1)}, bf16[24,4,3584]{2,1,0:T(4,128)(2,1)}, bf16[24,4,3584]{2,1,0:T(4,128)(2,1)}) custom-call(bf16[24,4,3584]{2,1,0:T(4,128)(2,1)} %copy-done.2, bf16[24,4,3584]{2,1,0:T(4,128)(2,1)} %collective-permute-done.6.refs_1_, ...), custom_call_target="tpu_custom_call" | custom-call | tf_op jit(solution)/shard_map/pallas_call | solution.py:315
  336.3 0.0 copy-start.1
  336.4 1.6 collective-permute-start.10
  338.0 2.8 collective-permute-start.8
  340.8 0.4 collective-permute-start.9
  341.2 8.8 %collective-permute-done.10.refs_3_ = bf16[24,4,3584]{2,1,0:T(4,128)(2,1)} collective-permute-done((bf16[24,4,3584]{2,1,0:T(4,128)(2,1)}, bf16[24,4,3584]{2,1,0:T(4,128)(2,1)}, u32[]{:S(2)}, u32[]{:S(2)}) %collective-permute-start.10) | collective-permute-done | bytes 688160 | tf_op jit(solution)/shard_map/ppermute | solution.py:311
  349.9 13.7 %collective-permute-done.8.refs_1_ = bf16[24,4,3584]{2,1,0:T(4,128)(2,1)} collective-permute-done((bf16[24,4,3584]{2,1,0:T(4,128)(2,1)}, bf16[24,4,3584]{2,1,0:T(4,128)(2,1)}, u32[]{:S(2)}, u32[]{:S(2)}) %collective-permute-start.8) | collective-permute-done | bytes 688160 | tf_op jit(solution)/shard_map/ppermute | solution.py:311
  363.7 15.6 %shard_map.111 = bf16[96,4,3584]{2,1,0:T(4,128)(2,1)} custom-call(bf16[24,4,3584]{2,1,0:T(4,128)(2,1)} %get-tuple-element.30.refs_0_, bf16[24,4,3584]{2,1,0:T(4,128)(2,1)} %collective-permute-done.8.refs_1_, bf16[24,4,3584]{2,1,0:T(4,128)(2,1)} %collective-permute-done.9.refs_2_, bf16[24,4,3584]{2,1,0:T(4,128)(2,1)} %collective-permute-done.10.refs_3_, ...), custom_call_target="tpu_custom_call" | custom-call | tf_op jit(solution)/shard_map/pallas_call | solution.py:335
  379.3 8.6 %all-to-all-start.2 = ((bf16[96,4,3584]{2,1,0:T(4,128)(2,1)}), bf16[96,4,3584]{2,1,0:T(4,128)(2,1)}, u32[]{:S(2)}, u32[]{:S(2)}) async-start(bf16[96,4,3584]{2,1,0:T(4,128)(2,1)} %shard_map.111), calls=%async_computation.2 | async-start | bytes 5505024 | tf_op jit(solution)/shard_map/all_to_all | solution.py:269
  387.9 12.2 %shard_map.106 = bf16[96,4,3584]{2,1,0:T(4,128)(2,1)} custom-call(bf16[96,4,3584]{2,1,0:T(4,128)(2,1)} %all-to-all-done.recv_ref, bf16[3584,512]{1,0:T(8,128)(2,1)} %bitcast.32, bf16[512,3584]{1,0:T(8,128)(2,1)} %bitcast.35, bf16[3584,512]{1,0:T(8,128)(2,1)} %collective-permute-done.2.up_other.refs_10_, ...), custom_call_target="tpu_custom_call" | custom-call | tf_op jit(solution)/shard_map/pallas_call | solution.py:335
  400.1 0.0 copy-start.5
  400.1 0.1 collective-permute-start.4
  400.2 42.0 %collective-permute-done.4 = bf16[96,4,3584]{2,1,0:T(4,128)(2,1)} collective-permute-done((bf16[96,4,3584]{2,1,0:T(4,128)(2,1)}, bf16[96,4,3584]{2,1,0:T(4,128)(2,1)}, u32[]{:S(2)}, u32[]{:S(2)}) %collective-permute-start.4) | collective-permute-done | bytes 2752544 | tf_op jit(solution)/shard_map/ppermute | solution.py:31
  442.2 9.1 %all-to-all-start.1 = ((bf16[96,4,3584]{2,1,0:T(4,128)(2,1)}), bf16[96,4,3584]{2,1,0:T(4,128)(2,1)}, u32[]{:S(2)}, u32[]{:S(2)}) async-start(bf16[96,4,3584]{2,1,0:T(4,128)(2,1)} %collective-permute-done.4), calls=%async_computation.1 | async-start | bytes 5505024 | tf_op jit(solution)/shard_map/all_to_all | solution.py:269
  451.3 0.0 copy-start.9
  451.4 0.6 pad_maximum_fusion.1.info_ref
  452.0 1.8 shard_map.108
  453.7 3.7 shard_map.112
  457.4 0.5 collective-permute-start.1
  457.9 1.7 collective-permute-start
  459.6 36.6 %collective-permute-done.info_ref = f32[4,128]{1,0:T(4,128)S(1)} collective-permute-done((f32[4,128]{1,0:T(4,128)S(1)}, f32[4,128]{1,0:T(4,128)S(1)}, u32[]{:S(2)}, u32[]{:S(2)}) %collective-permute-start) | collective-permute-done | bytes 2080 | tf_op jit(solution)/shard_map/ppermute | solution.py:31
  496.2 0.6 copy-done.7
  496.8 1.8 shard_map.104
  498.6 2.2 shard_map.113
  500.7 10.9 %all-to-all-done.1.back_ref = bf16[96,4,3584]{2,1,0:T(4,128)(2,1)} async-done(((bf16[96,4,3584]{2,1,0:T(4,128)(2,1)}), bf16[96,4,3584]{2,1,0:T(4,128)(2,1)}, u32[]{:S(2)}, u32[]{:S(2)}) %all-to-all-start.1) | async-done | bytes 2752544 | tf_op jit(solution)/shard_map/all_to_all | solution.py:269
  511.6 3.7 shard_map.107
  (31 shorter events, 0.1 us)
Async XLA Ops:
  4.3 375.0 %all-to-all-start = ((bf16[96,4,3584]{2,1,0:T(4,128)(2,1)}), bf16[96,4,3584]{2,1,0:T(4,128)(2,1)}, u32[]{:S(2)}, u32[]{:S(2)}) async-start(bf16[96,4,3584]{2,1,0:T(4,128)(2,1)} %bitcast.36), calls=%async_computation | async-start | bytes 5505024 | tf_op jit(solution)/shard_map/all_to_all | solution.py:269
  16.6 347.1 %collective-permute-start.2 = (bf16[3584,512]{1,0:T(8,128)(2,1)}, bf16[3584,512]{1,0:T(8,128)(2,1)}, u32[]{:S(2)}, u32[]{:S(2)}) collective-permute-start(bf16[3584,512]{1,0:T(8,128)(2,1)} %bitcast.30), channel_id=1, source_target_pairs={{0,1},{1,0},{2,3},{3,2},{4,5},{5,4},{6,7},{7,6},{8,9},{9,8},{10,11... | collective-permute-start | bytes 11010056 | tf_op jit(solution)/shard_map/ppermute | solution.py:26
  16.7 347.0 %collective-permute-start.3 = (bf16[512,3584]{1,0:T(8,128)(2,1)}, bf16[512,3584]{1,0:T(8,128)(2,1)}, u32[]{:S(2)}, u32[]{:S(2)}) collective-permute-start(bf16[512,3584]{1,0:T(8,128)(2,1)} %bitcast.33), channel_id=1, source_target_pairs={{0,1},{1,0},{2,3},{3,2},{4,5},{5,4},{6,7},{7,6},{8,9},{9,8},{10,11... | collective-permute-start | bytes 11010056 | tf_op jit(solution)/shard_map/ppermute | solution.py:26
  23.6 85.9 %collective-permute-start.11 = (bf16[24,4,3584]{2,1,0:T(4,128)(2,1)}, bf16[24,4,3584]{2,1,0:T(4,128)(2,1)S(1)}, u32[]{:S(2)}, u32[]{:S(2)}) collective-permute-start(bf16[24,4,3584]{2,1,0:T(4,128)(2,1)} %bitcast.55), channel_id=1, source_target_pairs={{0,8},{1,9},{2,10},{3,11},{4,12},{5,13},{6,14},{7,15},{8,16},{9,17... | collective-permute-start | bytes 2064392 | tf_op jit(solution)/shard_map/ppermute | solution.py:304
  26.0 84.8 %collective-permute-start.12 = (bf16[24,4,3584]{2,1,0:T(4,128)(2,1)}, bf16[24,4,3584]{2,1,0:T(4,128)(2,1)S(1)}, u32[]{:S(2)}, u32[]{:S(2)}) collective-permute-start(bf16[24,4,3584]{2,1,0:T(4,128)(2,1)} %bitcast.54), channel_id=1, source_target_pairs={{0,24},{1,25},{2,26},{3,27},{4,28},{5,29},{6,30},{7,31},{8,0},{9,1... | collective-permute-start | bytes 2064392 | tf_op jit(solution)/shard_map/ppermute | solution.py:304
  27.8 95.0 %collective-permute-start.13 = (bf16[24,4,3584]{2,1,0:T(4,128)(2,1)}, bf16[24,4,3584]{2,1,0:T(4,128)(2,1)}, u32[]{:S(2)}, u32[]{:S(2)}) collective-permute-start(bf16[24,4,3584]{2,1,0:T(4,128)(2,1)} %bitcast.53), channel_id=1, source_target_pairs={{0,4},{1,5},{2,6},{3,7},{4,8},{5,9},{6,10},{7,11},{8,12},{9,13},{1... | collective-permute-start | bytes 2064392 | tf_op jit(solution)/shard_map/ppermute | solution.py:304
  109.4 1.4 copy-start.3
  109.4 48.1 %collective-permute-start.14 = (bf16[24,4,3584]{2,1,0:T(4,128)(2,1)}, bf16[24,4,3584]{2,1,0:T(4,128)(2,1)}, u32[]{:S(2)}, u32[]{:S(2)}) collective-permute-start(bf16[24,4,3584]{2,1,0:T(4,128)(2,1)} %bitcast.52), channel_id=1, source_target_pairs={{0,28},{1,29},{2,30},{3,31},{4,0},{5,1},{6,2},{7,3},{8,4},{9,5},{1... | collective-permute-start | bytes 2064392 | tf_op jit(solution)/shard_map/ppermute | solution.py:304
  110.8 0.9 copy-start.4
  111.7 134.5 %collective-permute-start.5 = (bf16[24,4,3584]{2,1,0:T(4,128)(2,1)}, bf16[24,4,3584]{2,1,0:T(4,128)(2,1)S(1)}, u32[]{:S(2)}, u32[]{:S(2)}) collective-permute-start(bf16[24,4,3584]{2,1,0:T(4,128)(2,1)} %bitcast.51), channel_id=1, source_target_pairs={{0,16},{1,17},{2,18},{3,19},{4,20},{5,21},{6,22},{7,23},{8,24},{9,... | collective-permute-start | bytes 2064392 | tf_op jit(solution)/shard_map/ppermute | solution.py:304
  122.8 124.4 %collective-permute-start.6 = (bf16[24,4,3584]{2,1,0:T(4,128)(2,1)}, bf16[24,4,3584]{2,1,0:T(4,128)(2,1)}, u32[]{:S(2)}, u32[]{:S(2)}) collective-permute-start(bf16[24,4,3584]{2,1,0:T(4,128)(2,1)} %bitcast.50), channel_id=1, source_target_pairs={{0,12},{1,13},{2,14},{3,15},{4,16},{5,17},{6,18},{7,19},{8,20},{9,... | collective-permute-start | bytes 2064392 | tf_op jit(solution)/shard_map/ppermute | solution.py:304
  157.5 91.6 %collective-permute-start.7 = (bf16[24,4,3584]{2,1,0:T(4,128)(2,1)}, bf16[24,4,3584]{2,1,0:T(4,128)(2,1)}, u32[]{:S(2)}, u32[]{:S(2)}) collective-permute-start(bf16[24,4,3584]{2,1,0:T(4,128)(2,1)} %bitcast.49), channel_id=1, source_target_pairs={{0,20},{1,21},{2,22},{3,23},{4,24},{5,25},{6,26},{7,27},{8,28},{9,... | collective-permute-start | bytes 2064392 | tf_op jit(solution)/shard_map/ppermute | solution.py:304
  246.1 0.8 copy-start.2
  247.0 89.3 %collective-permute-start.15 = (bf16[24,4,3584]{2,1,0:T(4,128)(2,1)}, bf16[24,4,3584]{2,1,0:T(4,128)(2,1)S(1)}, u32[]{:S(2)}, u32[]{:S(2)}) collective-permute-start(bf16[24,4,3584]{2,1,0:T(4,128)(2,1)} %get-tuple-element.39), channel_id=1, source_target_pairs={{0,3},{1,2},{2,1},{3,0},{4,7},{5,6},{6,5},{7,4},{8,11},{9,10},{10,... | collective-permute-start | bytes 2064392 | tf_op jit(solution)/shard_map/ppermute | solution.py:311
  247.2 90.7 %collective-permute-start.16 = (bf16[24,4,3584]{2,1,0:T(4,128)(2,1)}, bf16[24,4,3584]{2,1,0:T(4,128)(2,1)}, u32[]{:S(2)}, u32[]{:S(2)}) collective-permute-start(bf16[24,4,3584]{2,1,0:T(4,128)(2,1)} %get-tuple-element.40), channel_id=1, source_target_pairs={{0,32},{1,33},{2,34},{3,35},{4,36},{5,37},{6,38},{7,39},{8,40},{9,... | collective-permute-start | bytes 2064392 | tf_op jit(solution)/shard_map/ppermute | solution.py:311
  249.1 91.7 %collective-permute-start.17 = (bf16[24,4,3584]{2,1,0:T(4,128)(2,1)}, bf16[24,4,3584]{2,1,0:T(4,128)(2,1)}, u32[]{:S(2)}, u32[]{:S(2)}) collective-permute-start(bf16[24,4,3584]{2,1,0:T(4,128)(2,1)} %get-tuple-element.41), channel_id=1, source_target_pairs={{0,35},{1,34},{2,33},{3,32},{4,39},{5,38},{6,37},{7,36},{8,43},{9,... | collective-permute-start | bytes 2064392 | tf_op jit(solution)/shard_map/ppermute | solution.py:311
  336.3 27.3 %copy-start.1 = (bf16[24,4,3584]{2,1,0:T(4,128)(2,1)}, bf16[24,4,3584]{2,1,0:T(4,128)(2,1)S(1)}, u32[]{:S(2)}) copy-start(bf16[24,4,3584]{2,1,0:T(4,128)(2,1)S(1)} %collective-permute-done.15.refs_5_) | copy-start | bytes 2064388
  336.4 13.5 %collective-permute-start.10 = (bf16[24,4,3584]{2,1,0:T(4,128)(2,1)}, bf16[24,4,3584]{2,1,0:T(4,128)(2,1)}, u32[]{:S(2)}, u32[]{:S(2)}) collective-permute-start(bf16[24,4,3584]{2,1,0:T(4,128)(2,1)} %get-tuple-element.33), channel_id=1, source_target_pairs={{0,35},{1,34},{2,33},{3,32},{4,39},{5,38},{6,37},{7,36},{8,43},{9,... | collective-permute-start | bytes 2064392 | tf_op jit(solution)/shard_map/ppermute | solution.py:311
  338.0 25.7 %collective-permute-start.8 = (bf16[24,4,3584]{2,1,0:T(4,128)(2,1)}, bf16[24,4,3584]{2,1,0:T(4,128)(2,1)}, u32[]{:S(2)}, u32[]{:S(2)}) collective-permute-start(bf16[24,4,3584]{2,1,0:T(4,128)(2,1)} %get-tuple-element.31), channel_id=1, source_target_pairs={{0,3},{1,2},{2,1},{3,0},{4,7},{5,6},{6,5},{7,4},{8,11},{9,10},{10,... | collective-permute-start | bytes 2064392 | tf_op jit(solution)/shard_map/ppermute | solution.py:311
  340.8 22.9 %collective-permute-start.9 = (bf16[24,4,3584]{2,1,0:T(4,128)(2,1)}, bf16[24,4,3584]{2,1,0:T(4,128)(2,1)}, u32[]{:S(2)}, u32[]{:S(2)}) collective-permute-start(bf16[24,4,3584]{2,1,0:T(4,128)(2,1)} %get-tuple-element.32), channel_id=1, source_target_pairs={{0,32},{1,33},{2,34},{3,35},{4,36},{5,37},{6,38},{7,39},{8,40},{9,... | collective-permute-start | bytes 2064392 | tf_op jit(solution)/shard_map/ppermute | solution.py:311
  379.3 63.0 %all-to-all-start.2 = ((bf16[96,4,3584]{2,1,0:T(4,128)(2,1)}), bf16[96,4,3584]{2,1,0:T(4,128)(2,1)}, u32[]{:S(2)}, u32[]{:S(2)}) async-start(bf16[96,4,3584]{2,1,0:T(4,128)(2,1)} %shard_map.111), calls=%async_computation.2 | async-start | bytes 5505024 | tf_op jit(solution)/shard_map/all_to_all | solution.py:269
  400.1 51.2 %copy-start.5 = (s32[1,128,2]{1,2,0:T(2,128)S(1)}, s32[1,128,2]{1,2,0:T(2,128)}, u32[]{:S(2)}) copy-start(s32[1,128,2]{1,2,0:T(2,128)} %param.14) | copy-start | bytes 3076
  400.1 51.2 %copy-start.8 = (f32[1,128,2]{1,2,0:T(2,128)S(1)}, f32[1,128,2]{1,2,0:T(2,128)}, u32[]{:S(2)}) copy-start(f32[1,128,2]{1,2,0:T(2,128)} %param.15) | copy-start | bytes 3076
  400.1 42.1 %collective-permute-start.4 = (bf16[96,4,3584]{2,1,0:T(4,128)(2,1)}, bf16[96,4,3584]{2,1,0:T(4,128)(2,1)}, u32[]{:S(2)}, u32[]{:S(2)}) collective-permute-start(bf16[96,4,3584]{2,1,0:T(4,128)(2,1)} %shard_map.106), channel_id=1, source_target_pairs={{0,64},{64,128},{128,192},{192,0},{1,65},{65,129},{129,193},{193,1... | collective-permute-start | bytes 8257544 | tf_op jit(solution)/shard_map/ppermute | solution.py:31
  442.2 69.4 %all-to-all-start.1 = ((bf16[96,4,3584]{2,1,0:T(4,128)(2,1)}), bf16[96,4,3584]{2,1,0:T(4,128)(2,1)}, u32[]{:S(2)}, u32[]{:S(2)}) async-start(bf16[96,4,3584]{2,1,0:T(4,128)(2,1)} %collective-permute-done.4), calls=%async_computation.1 | async-start | bytes 5505024 | tf_op jit(solution)/shard_map/all_to_all | solution.py:269
  451.3 6.6 %copy-start.6 = (s32[1,128,2]{1,2,0:T(2,128)S(1)}, s32[1,128,2]{1,2,0:T(2,128)}, u32[]{:S(2)}) copy-start(s32[1,128,2]{1,2,0:T(2,128)} %param.10) | copy-start | bytes 3076
  451.3 6.6 %copy-start.9 = (f32[1,128,2]{1,2,0:T(2,128)S(1)}, f32[1,128,2]{1,2,0:T(2,128)}, u32[]{:S(2)}) copy-start(f32[1,128,2]{1,2,0:T(2,128)} %param.11) | copy-start | bytes 3076
  457.4 41.2 %collective-permute-start.18 = (bf16[128,3584]{1,0:T(8,128)(2,1)}, bf16[128,3584]{1,0:T(8,128)(2,1)}, u32[]{:S(2)}, u32[]{:S(2)}) collective-permute-start(bf16[128,3584]{1,0:T(8,128)(2,1)} %shard_map.112), channel_id=1, source_target_pairs={{0,192},{64,0},{128,64},{192,128},{1,193},{65,1},{129,65},{193,129... | collective-permute-start | bytes 2752520 | tf_op jit(solution)/shard_map/ppermute | solution.py:31
  457.4 43.3 %collective-permute-start.1 = (bf16[128,3584]{1,0:T(8,128)(2,1)}, bf16[128,3584]{1,0:T(8,128)(2,1)S(1)}, u32[]{:S(2)}, u32[]{:S(2)}) collective-permute-start(bf16[128,3584]{1,0:T(8,128)(2,1)} %bitcast.43), channel_id=1, source_target_pairs={{0,64},{64,128},{128,192},{192,0},{1,65},{65,129},{129,193},{193,1... | collective-permute-start | bytes 2752520 | tf_op jit(solution)/shard_map/ppermute | solution.py:31
  457.9 38.3 %collective-permute-start = (f32[4,128]{1,0:T(4,128)S(1)}, f32[4,128]{1,0:T(4,128)S(1)}, u32[]{:S(2)}, u32[]{:S(2)}) collective-permute-start(f32[4,128]{1,0:T(4,128)S(1)} %pad_maximum_fusion), channel_id=1, source_target_pairs={{0,64},{64,128},{128,192},{192,0},{1,65},{65,129},{129,193},{193,1... | collective-permute-start | bytes 6152 | tf_op jit(solution)/shard_map/ppermute | solution.py:31
  496.2 0.6 copy-start.7
  500.7 10.9 %copy-start = (bf16[128,3584]{1,0:T(8,128)(2,1)}, bf16[128,3584]{1,0:T(8,128)(2,1)S(1)}, u32[]{:S(2)}) copy-start(bf16[128,3584]{1,0:T(8,128)(2,1)S(1)} %collective-permute-done.1.x_ref) | copy-start | bytes 2752516
